TPU v7x, 8 devices: a whole 2x2x1 slice. The times are simulated.
8 devices in a mesh: data: 8 (over z, y, x, core).
Axes of the slice: x: 2, y: 2, z: 1, core: 2. Of those that a mesh axis runs over, the one named last changes fastest.
Arguments:
- w_in: float32 [8192, 2048], replicated
- w_up: float32 [2, 2048, 8192], replicated
- w_down: float32 [2, 8192, 2048], replicated
- mom_in: float32 [8192, 2048], replicated
- mom_up: float32 [2, 2048, 8192], replicated
- mom_down: float32 [2, 8192, 2048], replicated
- x_now: bfloat16 [4096, 8192], P('data')
- y_now: bfloat16 [4096, 2048], P('data')
- x_next: bfloat16 [4096, 8192], P('data')
- y_next: bfloat16 [4096, 2048], P('data')
Outputs:
- output 1: float32 [8192, 2048], replicated
- output 2: float32 [2, 2048, 8192], replicated
- output 3: float32 [2, 8192, 2048], replicated
- output 4: float32 [8192, 2048], replicated
- output 5: float32 [2, 2048, 8192], replicated
- output 6: float32 [2, 8192, 2048], replicated
- output 7: float32 [4096], P('data')
- output 8: float32 [4096, 2048], P('data')
All inputs are finite; a program needn't handle non-finite values.
Results may differ from a plain program's by a relative error of at most 0.0113557.
Values are sent between devices in bfloat16 or wider.
A program may use at most 5.25 GiB of HBM per device.

v0:
```python
import jax
import jax.numpy as jnp
from jax import lax
from jax.sharding import PartitionSpec as P

MOMENTUM = 0.9
ROW_CONTRACT = (((0,), (0,)), ((), ()))
COL_CONTRACT = (((1,), (1,)), ((), ()))


def gelu_tanh(pre_value):
    return jax.nn.gelu(pre_value, approximate=True)


def stack_forward(x_rows, in_low, up_low, down_low):
    h_state = jnp.dot(x_rows, in_low, preferred_element_type=jnp.float32)
    saved_acts = []
    for layer_idx in range(up_low.shape[0]):
        h_low = h_state.astype(jnp.bfloat16)
        pre_act = jnp.dot(h_low, up_low[layer_idx], preferred_element_type=jnp.float32)
        act_val, gelu_back = jax.vjp(gelu_tanh, pre_act)
        act_low = act_val.astype(jnp.bfloat16)
        h_state = h_state + jnp.dot(act_low, down_low[layer_idx], preferred_element_type=jnp.float32)
        saved_acts.append((h_low, act_low, gelu_back))
    return h_state, saved_acts


def solution(mesh):
    group_size = mesh.shape["data"]

    def device_steps(w_in, w_up, w_down, mom_in, mom_up, mom_down, x_now, y_now, x_next, y_next):
        local_rows, model_width = y_now.shape
        layer_count = w_up.shape[0]
        step_size = 4.0 * model_width / (w_up.shape[2] * (layer_count + 1))
        up_low = w_up.astype(jnp.bfloat16)
        down_low = w_down.astype(jnp.bfloat16)
        h_last, saved_acts = stack_forward(x_now, w_in.astype(jnp.bfloat16), up_low, down_low)
        cot_state = (h_last - y_now.astype(jnp.float32)) / (local_rows * group_size * model_width)
        grads_up = [None] * layer_count
        grads_down = [None] * layer_count
        for layer_idx in reversed(range(layer_count)):
            h_low, act_low, gelu_back = saved_acts[layer_idx]
            cot_low = cot_state.astype(jnp.bfloat16)
            local_down = lax.dot_general(act_low, cot_low, ROW_CONTRACT, preferred_element_type=jnp.float32)
            grads_down[layer_idx] = lax.psum(local_down.astype(jnp.bfloat16), "data")
            act_cot = lax.dot_general(cot_low, down_low[layer_idx], COL_CONTRACT, preferred_element_type=jnp.float32)
            pre_cot = gelu_back(act_cot)[0].astype(jnp.bfloat16)
            local_up = lax.dot_general(h_low, pre_cot, ROW_CONTRACT, preferred_element_type=jnp.float32)
            grads_up[layer_idx] = lax.psum(local_up.astype(jnp.bfloat16), "data")
            cot_state = cot_state + lax.dot_general(pre_cot, up_low[layer_idx], COL_CONTRACT, preferred_element_type=jnp.float32)
        local_in = lax.dot_general(x_now, cot_state.astype(jnp.bfloat16), ROW_CONTRACT, preferred_element_type=jnp.float32)
        grad_in = lax.psum(local_in.astype(jnp.bfloat16), "data")
        new_mom_in = MOMENTUM * mom_in + grad_in.astype(jnp.float32)
        new_mom_up = MOMENTUM * mom_up + jnp.stack(grads_up).astype(jnp.float32)
        new_mom_down = MOMENTUM * mom_down + jnp.stack(grads_down).astype(jnp.float32)
        new_w_in = w_in - step_size * new_mom_in
        new_w_up = w_up - step_size * new_mom_up
        new_w_down = w_down - step_size * new_mom_down
        h_next = stack_forward(x_next, new_w_in.astype(jnp.bfloat16), new_w_up.astype(jnp.bfloat16), new_w_down.astype(jnp.bfloat16))[0]
        loss_next = jnp.sum(jnp.square(h_next - y_next.astype(jnp.float32)), axis=1) / (2 * model_width)
        return (new_w_in, new_w_up, new_w_down, new_mom_in, new_mom_up, new_mom_down, loss_next, h_next)

    param_spec = P()
    row_spec = P("data", None)
    return jax.shard_map(
        device_steps,
        mesh=mesh,
        in_specs=(param_spec,) * 6 + (row_spec,) * 4,
        out_specs=(param_spec,) * 6 + (P("data"), row_spec),
        check_vma=False,
    )
```

profile of v0, /device:TPU:1, one launch (start us, length us, event | category | flops | bytes accessed | tf_op | source)
XLA Modules:
  0.0 2843.7 jit_solution(9960915258319441776)
XLA Ops:
  7.2 63.5 %convert_element_type.92 = bf16[2,2048,8192]{2,1,0:T(8,128)(2,1)} convert(f32[2,2048,8192]{2,1,0:T(8,128)} %param.11) | non-fusion elementwise | flops 33554432 | bytes 201326592 | tf_op jit(solution)/shard_map/convert_element_type | solution.py:35
  70.8 63.6 %convert_element_type.94 = bf16[2,8192,2048]{2,1,0:T(8,128)(2,1)} convert(f32[2,8192,2048]{2,1,0:T(8,128)} %param.12) | non-fusion elementwise | flops 33554432 | bytes 201326592 | tf_op jit(solution)/shard_map/convert_element_type | solution.py:36
  134.4 29.7 %fusion.6 = f32[512,2048]{1,0:T(8,128)} fusion(bf16[512,8192]{1,0:T(8,128)(2,1)} %param.16, f32[8192,2048]{1,0:T(8,128)} %param.10), kind=kOutput, calls=%fused_computation.25 | convolution fusion | flops 17196646400 | bytes 79691776 | tf_op jit(solution)/shard_map/dot_general | solution.py:16
  164.1 26.2 fusion.9
  190.3 28.2 fusion.56
  218.5 26.4 fusion.13
  244.8 28.6 %subtract_multiply_fusion = f32[512,2048]{1,0:T(8,128)} fusion(bf16[512,2048]{1,0:T(8,128)(2,1)S(1)} %copy-done.2, f32[512,2048]{1,0:T(8,128)} %fusion.56, bf16[2,8192,2048]{2,1,0:T(8,128)(2,1)} %convert_element_type.94, f32[512,8192]{1,0:T(8,128)} %fusion.13), kind=kOutput, calls=%fused_computation.85 | convolution fusion | flops 17221812224 | bytes 60817408 | tf_op jit(solution)/shard_map/dot_general | solution.py:23
  273.5 33.6 %fusion.29 = bf16[512,8192]{1,0:T(8,128)(2,1)} fusion(f32[512,8192]{1,0:T(8,128)} %fusion.13, bf16[2,8192,2048]{2,1,0:T(8,128)(2,1)} %convert_element_type.94, f32[512,2048]{1,0:T(8,128)} %subtract_multiply_fusion), kind=kOutput, calls=%fused_computation.54 | convolution fusion | flops 17264803840 | bytes 62914560 | tf_op jit(solution)/shard_map/dot_general | solution.py:46
  307.1 27.7 convert_bitcast_fusion
  361.0 26.3 convert_bitcast_fusion.1
  413.1 33.6 %fusion.22 = bf16[512,8192]{1,0:T(8,128)(2,1)} fusion(f32[512,8192]{1,0:T(8,128)} %fusion.9, bf16[2,8192,2048]{2,1,0:T(8,128)(2,1)} %convert_element_type.94, f32[512,2048]{1,0:T(8,128)} %copy-done.4), kind=kOutput, calls=%fused_computation.47 | convolution fusion | flops 17264803840 | bytes 62914560 | tf_op jit(solution)/shard_map/dot_general | solution.py:46
  521.9 61.3 %copy.19 = f32[8192,2048]{0,1:T(8,128)} copy(f32[8192,2048]{1,0:T(8,128)} %param.10) | data formatting | bytes 134217728 | tf_op args[0]
  585.7 61.2 %copy.18 = f32[8192,2048]{0,1:T(8,128)} copy(f32[8192,2048]{1,0:T(8,128)} %param.13) | data formatting | bytes 134217728 | tf_op args[3]
  646.9 489.2 %all-reduce.7.cloned.1.call-done = (bf16[1,8192,2048]{2,1,0:T(8,128)(2,1)}, bf16[1,8192,2048]{2,1,0:T(8,128)(2,1)}) async-done(((bf16[1,8192,2048]{2,1,0:T(8,128)(2,1)}, bf16[1,8192,2048]{2,1,0:T(8,128)(2,1)}), (bf16[1,8192,2048]{2,1,0:T(8,128)(2,1)}, bf16[1,8192,2048]{2,1,0:T(8,128)(2,1)})) %all-reduce.7.cloned.1.call-update) | async-done | bytes 67108880 | tf_op jit(solution)/shard_map/psum | solution.py:45
  1136.0 213.4 %fusion.77 = (bf16[2,8192,2048]{2,1,0:T(8,128)(2,1)}, f32[2,8192,2048]{2,1,0:T(8,128)}, f32[2,8192,2048]{2,1,0:T(8,128)}) fusion(f32[2,8192,2048]{2,1,0:T(8,128)} %param.12, bf16[1,8192,2048]{2,1,0:T(8,128)(2,1)} %get-tuple-element.19, bf16[1,8192,2048]{2,1,0:T(8,128)(2,1)} %get-tuple-element.20, f32[2,8192,2048]{2,1,0:T(8,128)} %param.15), kind=kLoop, calls=%fused_computation.108 | loop fusion | flops 234881024 | bytes 671088640 | tf_op jit(solution)/shard_map/convert_element_type | solution.py:59
  1349.4 903.2 %all-reduce.5.cloned.1.call-done = (bf16[8192,2048]{0,1:T(8,128)(2,1)}, bf16[1,2048,8192]{2,1,0:T(8,128)(2,1)}, bf16[1,2048,8192]{2,1,0:T(8,128)(2,1)}) async-done(((bf16[8192,2048]{0,1:T(8,128)(2,1)}, bf16[1,2048,8192]{2,1,0:T(8,128)(2,1)}, bf16[1,2048,8192]{2,1,0:T(8,128)(2,1)}), (bf16[8192,2048]{0,1:T(8,128)(2,1)}, bf16[1,2048,8192]{2,1,0:T(8,128)(2,1)}, ...) | async-done | bytes 100663312 | tf_op jit(solution)/shard_map/psum | solution.py:52
  2252.6 95.6 %multiply_subtract_fusion.2 = (f32[8192,2048]{0,1:T(8,128)}, f32[8192,2048]{0,1:T(8,128)}) fusion(f32[8192,2048]{0,1:T(8,128)} %copy.19, bf16[8192,2048]{0,1:T(8,128)(2,1)} %get-tuple-element.16, f32[8192,2048]{0,1:T(8,128)} %copy.18), kind=kLoop, calls=%fused_computation.4 | loop fusion | flops 83886080 | bytes 301989888 | tf_op jit(solution)/shard_map/sub | solution.py:56
  2348.2 66.0 %copy.24 = f32[8192,2048]{1,0:T(8,128)} copy(f32[8192,2048]{0,1:T(8,128)} %get-tuple-element.28) | data formatting | bytes 134217728
  2414.2 66.0 %copy.23 = f32[8192,2048]{1,0:T(8,128)} copy(f32[8192,2048]{0,1:T(8,128)} %get-tuple-element.27) | data formatting | bytes 134217728
  2480.2 29.7 %fusion.4 = f32[2048,512]{1,0:T(8,128)} fusion(bf16[512,8192]{1,0:T(8,128)(2,1)} %param.18, f32[8192,2048]{0,1:T(8,128)} %get-tuple-element.27), kind=kOutput, calls=%fused_computation.18 | convolution fusion | flops 17196646400 | bytes 79691776 | tf_op jit(solution)/shard_map/dot_general | solution.py:16
  2509.9 209.9 %fusion.76 = (bf16[2,2048,8192]{2,1,0:T(8,128)(2,1)}, f32[2,2048,8192]{2,1,0:T(8,128)}, f32[2,2048,8192]{2,1,0:T(8,128)}) fusion(f32[2,2048,8192]{2,1,0:T(8,128)} %param.11, bf16[1,2048,8192]{2,1,0:T(8,128)(2,1)} %get-tuple-element.17, bf16[1,2048,8192]{2,1,0:T(8,128)(2,1)} %get-tuple-element.18, f32[2,2048,8192]{2,1,0:T(8,128)} %param.14), kind=kLoop, calls=%fused_computation.107 | loop fusion | flops 234881024 | bytes 671088640 | tf_op jit(solution)/shard_map/convert_element_type | solution.py:59
  2719.8 28.9 %fusion.37.clone.7 = bf16[512,8192]{1,0:T(8,128)(2,1)} fusion(bf16[2,2048,8192]{2,1,0:T(8,128)(2,1)} %get-tuple-element.21, f32[2048,512]{1,0:T(8,128)S(1)} %copy-done.3), kind=kOutput, calls=%fused_computation.62.clone.clone.clone.clone.clone.2 | convolution fusion | flops 17217617920 | bytes 46137344 | tf_op jit(solution)/shard_map/dot_general | solution.py:20
  2774.2 30.2 %fusion.45.clone.3.clone.5 = bf16[512,8192]{1,0:T(8,128)(2,1)} fusion(bf16[2,2048,8192]{2,1,0:T(8,128)(2,1)} %get-tuple-element.21, f32[512,2048]{0,1:T(8,128)} %bitcast_add_fusion), kind=kOutput, calls=%fused_computation.70.clone.clone.clone.clone.clone.clone.clone.2 | convolution fusion | flops 17218666496 | bytes 46137344 | tf_op jit(solution)/shard_map/dot_general | solution.py:20
  2804.4 26.4 multiply_reduce_fusion
  (25 shorter events, 160.9 us)
Async XLA Ops:
  7.2 1128.9 %all-reduce.7.cloned.1.call-start = ((), (), s32[]{:S(2)}) async-start(), calls=%async_computation.1 | async-start | bytes 134217728 | tf_op jit(solution)/shard_map/psum | solution.py:45
  218.5 26.4 copy-start.2
  359.1 2.0 copy-start.4
  387.4 1865.3 %all-reduce.5.cloned.1.call-start = ((), (), s32[]{:S(2)}) async-start(), calls=%async_computation | async-start | bytes 201326592 | tf_op jit(solution)/shard_map/psum | solution.py:52
  446.7 25.9 copy-start.5
  521.8 61.4 %copy-start = (bf16[512,2048]{1,0:T(8,128)(2,1)S(1)}, bf16[512,2048]{1,0:T(8,128)(2,1)}, u32[]{:S(2)}) copy-start(bf16[512,2048]{1,0:T(8,128)(2,1)} %param.19) | copy-start | bytes 6291460
  2509.9 209.9 %copy-start.3 = (f32[2048,512]{1,0:T(8,128)S(1)}, f32[2048,512]{1,0:T(8,128)}, u32[]{:S(2)}) copy-start(f32[2048,512]{1,0:T(8,128)} %fusion.4) | copy-start | bytes 12582916
  2774.2 30.2 %copy-start.1 = (bf16[512,2048]{0,1:T(8,128)(2,1)S(1)}, bf16[512,2048]{0,1:T(8,128)(2,1)}, u32[]{:S(2)}) copy-start(bf16[512,2048]{0,1:T(8,128)(2,1)} %copy.22) | copy-start | bytes 6291460
Sparse Core Ops, SparseCore 0:
  387.5 748.4 all-reduce.6
  1140.9 1111.7 all-reduce.4
where the time goes:
time: 2850 us; the launch traced here: 2840 us
  waiting for transfers between devices  1390 us (49%)
  other arithmetic  647 us (23%)
  matrix products  526 us (18%)
  local copies, waits for them, and re-layouts  264 us (9%)
    psum x1, waiting for transfers between devices, device_steps(): grad_in = lax.psum(local_in.astype(jnp.bfloat16), 'data')  903 us
    psum x1, waiting for transfers between devices, device_steps(): grads_down[layer_idx] = lax.psum(local_down.astype(jnp.bfloat16), 'data')  489 us
    unnamed x18, local copies, waits for them, and re-layouts  264 us
    convert_element_type x1, other arithmetic, device_steps(): new_w_down.astype(jnp.bfloat16)  213 us
    convert_element_type x1, other arithmetic, device_steps(): new_w_up.astype(jnp.bfloat16)  210 us
    dot_general x4, matrix products, stack_forward(): jnp.dot(h_low, up_low[layer_idx], preferred_element_type=jnp.float32)  112 us
    dot_general x4, matrix products, stack_forward(): jnp.dot(act_low, down_low[layer_idx], preferred_element_type=jnp.float32)  109 us
    sub x1, other arithmetic, device_steps(): new_w_in = w_in - step_size * new_mom_in  95.6 us
  transfers between devices with their start and end apart: 2, of which 2 were waited for; matrix products, arithmetic and copies ran while one was open for 17% of the time, Pallas kernels for 0%

commit v1 on v0

v1 whole, which is shorter than its diff:
```python
import functools

import jax
import jax.numpy as jnp
from jax import lax
from jax.experimental import pallas as pl
from jax.experimental.pallas import tpu as pltpu
from jax.sharding import PartitionSpec as P


MOMENTUM = 0.9
BLOCK = 256
STEP_BLOCK = 1024
CHUNK = 256
ROW_CONTRACT = (((0,), (0,)), ((), ()))
COL_CONTRACT = (((1,), (1,)), ((), ()))


def gelu_tanh(pre_value):
    return jax.nn.gelu(pre_value, approximate=True)


class Plan:
    def __init__(self, first, second, size):
        self.first, self.second, self.size = first, second, size
        me = lax.axis_index("data")
        bit = lambda mask: (me // mask) % 2
        self.f, self.s, self.c = bit(first), bit(second), bit(1)

    def quarter(self, flip_f, flip_c):
        f = 1 - self.f if flip_f else self.f
        c = 1 - self.c if flip_c else self.c
        return 2 * f + c

    def piece(self, flip_f, flip_s, flip_c):
        s = 1 - self.s if flip_s else self.s
        return 2 * self.quarter(flip_f, flip_c) + s

    def quarters(self):
        return [self.quarter(1, 0), self.quarter(1, 1), self.quarter(0, 1), self.quarter(0, 0)]

    def hop(self, value, mask):
        return lax.ppermute(value, "data", [(i, i ^ mask) for i in range(self.size)])

    def exchange_wide(self, parts):
        near, across, partner, own = parts
        near = self.hop(near, self.first)
        across = self.hop(across, self.first | 1)
        return [own, self.hop(partner, 1), near, across]

    def exchange_narrow(self, narrow):
        near = self.hop(narrow, self.first)
        return [narrow, self.hop(narrow, 1), near, self.hop(near, 1)]

    def reduce_piece(self, quarter_sum, axis):
        width = quarter_sum.shape[axis] // 2
        send = lax.dynamic_slice_in_dim(quarter_sum, (1 - self.s) * width, width, axis)
        keep = lax.dynamic_slice_in_dim(quarter_sum, self.s * width, width, axis)
        other = self.hop(send, self.second)
        return (keep.astype(jnp.float32) + other.astype(jnp.float32)).astype(jnp.bfloat16)

    def gather(self, own):
        s1 = self.hop(own, self.second)
        f0 = self.hop(own, self.first)
        f1 = self.hop(s1, self.first)
        near = [own, s1, f0, f1]
        far = [self.hop(value, 1) for value in near]
        flips = [(0, 0), (0, 1), (1, 0), (1, 1)]
        tagged = [(near[i], self.piece(*flips[i], 0)) for i in range(4)]
        tagged += [(far[i], self.piece(*flips[i], 1)) for i in range(4)]
        return [[tagged[i] for i in pair] for pair in ((0, 4), (1, 2), (5, 6), (3, 7))]


def run(kernel, table, operands, in_specs, out_shape, out_specs, steps, work, scratch=(), aliases=None):
    return pl.pallas_call(
        kernel,
        grid_spec=pltpu.PrefetchScalarGridSpec(
            num_scalar_prefetch=1, grid=(steps,), in_specs=in_specs, out_specs=out_specs, scratch_shapes=list(scratch)
        ),
        out_shape=out_shape,
        input_output_aliases=aliases or {},
        compiler_params=pltpu.CompilerParams(dimension_semantics=("arbitrary",)),
        cost_estimate=pl.CostEstimate(flops=work[0], bytes_accessed=work[1], transcendentals=0),
    )(table, *operands)


def lower(ref):
    return ref[...].reshape(ref.shape[-2:]).astype(jnp.bfloat16)


def store_part(step, per, part_refs, value):
    for idx, ref in enumerate(part_refs):

        @pl.when((step >= idx * per) & (step < (idx + 1) * per))
        def _(ref=ref):
            ref[...] = value


def part_specs(count, per, shape, axis):
    def at(idx):
        def block(i, t):
            place = jnp.clip(i - idx * per, 0, per - 1)
            return (place, 0) if axis == 0 else (0, place)

        return block

    return [pl.BlockSpec(shape, at(idx)) for idx in range(count)]


def split_kernel(table_ref, x_ref, *out_refs):
    store_part(pl.program_id(0), 1, out_refs, x_ref[...])


def split_cols(x, table, width):
    rows, count = x.shape[0], table.shape[0]
    shape = (rows, width)
    return run(
        split_kernel, table, [x],
        [pl.BlockSpec(shape, lambda i, t: (0, t[i]))],
        [jax.ShapeDtypeStruct(shape, x.dtype)] * count,
        part_specs(count, 1, shape, 1),
        count, (0, 4 * x.size),
    )


def up_kernel(per, table_ref, p_ref, w_ref, u_ref, *act_refs):
    values = []
    for lo in range(0, STEP_BLOCK, CHUNK):
        low = w_ref[0, :, lo : lo + CHUNK].astype(jnp.bfloat16)
        pre = jnp.dot(p_ref[...], low, preferred_element_type=jnp.float32)
        u_ref[:, lo : lo + CHUNK] = pre
        values.append(gelu_tanh(pre).astype(jnp.bfloat16))
    store_part(pl.program_id(0), per, act_refs, jnp.concatenate(values, axis=1))


def up_forward(p, w, layer, quarters):
    (rows, depth), inner = p.shape, w.shape[2]
    per = inner // 4 // STEP_BLOCK
    block = lambda i, t: t[i // per] * per + i % per
    return run(
        functools.partial(up_kernel, per), jnp.stack(quarters), [p, w],
        [
            pl.BlockSpec((rows, depth), lambda i, t: (0, 0)),
            pl.BlockSpec((1, depth, STEP_BLOCK), lambda i, t: (layer, 0, block(i, t))),
        ],
        [jax.ShapeDtypeStruct((rows, inner), jnp.float32)] + [jax.ShapeDtypeStruct((rows, inner // 4), jnp.bfloat16)] * 4,
        [pl.BlockSpec((rows, STEP_BLOCK), lambda i, t: (0, block(i, t)))] + part_specs(4, per, (rows, STEP_BLOCK), 1),
        4 * per, (2 * rows * depth * inner, 4 * depth * inner + 6 * rows * inner),
    )


def dot_nt(lhs, rhs):
    return lax.dot_general(lhs, rhs, COL_CONTRACT, preferred_element_type=jnp.float32)


def back_kernel(per, table_ref, c_ref, w_ref, u_ref, *q_refs):
    values = []
    for lo in range(0, STEP_BLOCK, CHUNK):
        act_cot = dot_nt(c_ref[...], w_ref[0, lo : lo + CHUNK, :].astype(jnp.bfloat16))
        gelu_back = jax.vjp(gelu_tanh, u_ref[:, lo : lo + CHUNK])[1]
        values.append(gelu_back(act_cot)[0].astype(jnp.bfloat16))
    store_part(pl.program_id(0), per, q_refs, jnp.concatenate(values, axis=1))


def down_backward(c, w, layer, u, quarters):
    (rows, width), inner = c.shape, w.shape[1]
    per = inner // 4 // STEP_BLOCK
    block = lambda i, t: t[i // per] * per + i % per
    return run(
        functools.partial(back_kernel, per), jnp.stack(quarters), [c, w, u],
        [
            pl.BlockSpec((rows, width), lambda i, t: (0, 0)),
            pl.BlockSpec((1, STEP_BLOCK, width), lambda i, t: (layer, block(i, t), 0)),
            pl.BlockSpec((rows, STEP_BLOCK), lambda i, t: (0, block(i, t))),
        ],
        [jax.ShapeDtypeStruct((rows, inner // 4), jnp.bfloat16)] * 4,
        part_specs(4, per, (rows, STEP_BLOCK), 1),
        4 * per, (2 * rows * width * inner, 4 * width * inner + 6 * rows * inner),
    )


def add_kernel(per, transposed, table_ref, base_ref, w_ref, *refs):
    *part_refs, out_ref = refs
    step = pl.program_id(0)

    @pl.when(step == 0)
    def _():
        out_ref[...] = base_ref[...]

    lhs = select_piece(step, per, part_refs)
    if transposed:
        out_ref[...] += dot_nt(lhs, lower(w_ref))
    else:
        out_ref[...] += jnp.dot(lhs, lower(w_ref), preferred_element_type=jnp.float32)


def add_product(base, parts, w, layer, quarters, transposed):
    rows, width = base.shape
    inner = 4 * parts[0].shape[1]
    per = inner // 4 // STEP_BLOCK
    block = lambda i, t: t[i // per] * per + i % per
    whole = pl.BlockSpec((rows, width), lambda i, t: (0, 0))
    if transposed:
        w_spec = pl.BlockSpec((1, width, STEP_BLOCK), lambda i, t: (layer, 0, block(i, t)))
    else:
        w_spec = pl.BlockSpec((1, STEP_BLOCK, width), lambda i, t: (layer, block(i, t), 0))
    return run(
        functools.partial(add_kernel, per, transposed), jnp.stack(quarters), [base, w, *parts],
        [whole, w_spec] + part_specs(4, per, (rows, STEP_BLOCK), 1),
        jax.ShapeDtypeStruct((rows, width), jnp.float32),
        whole,
        4 * per, (2 * rows * width * inner, 4 * width * inner + 2 * rows * inner),
    )


def in_kernel(table_ref, x_ref, w_ref, out_ref):
    term = jnp.dot(x_ref[...], lower(w_ref), preferred_element_type=jnp.float32)

    @pl.when(pl.program_id(0) == 0)
    def _():
        out_ref[...] = term

    @pl.when(pl.program_id(0) != 0)
    def _():
        out_ref[...] += term


def in_forward(x, w, table):
    (rows, depth), width = x.shape, w.shape[1]
    return run(
        in_kernel, table, [x, w],
        [pl.BlockSpec((rows, STEP_BLOCK), lambda i, t: (0, i)), pl.BlockSpec((STEP_BLOCK, width), lambda i, t: (i, 0))],
        jax.ShapeDtypeStruct((rows, width), jnp.float32),
        pl.BlockSpec((rows, width), lambda i, t: (0, 0)),
        depth // STEP_BLOCK, (2 * rows * depth * width, 4 * depth * width + 2 * rows * depth),
    )


def select_piece(step, steps_per_piece, piece_refs):
    value = piece_refs[0][...]
    for idx in range(1, len(piece_refs)):
        value = jnp.where(step >= idx * steps_per_piece, piece_refs[idx][...], value)
    return value


def updated(w_ref, m_ref, grad, step_size):
    new_m = MOMENTUM * m_ref[...] + grad.astype(jnp.float32).reshape(m_ref.shape)
    new_w = w_ref[...] - step_size * new_m
    return new_w, new_m


def rows_kernel(count, per, step_size, has_h, has_old, *refs):
    refs = list(refs)
    refs.pop(0)
    x_ref = refs.pop(0)
    w_ref, m_ref = refs.pop(0), refs.pop(0)
    pieces = [refs.pop(0) for _ in range(count)]
    h_ref = refs.pop(0) if has_h else None
    if has_old:
        refs.pop(0), refs.pop(0)
    new_w_ref, new_m_ref, out_ref = refs
    step = pl.program_id(0)
    new_w, new_m = updated(w_ref, m_ref, select_piece(step, per, pieces), step_size)
    new_w_ref[...] = new_w
    new_m_ref[...] = new_m
    low = new_w.reshape(new_w.shape[-2:]).astype(jnp.bfloat16)
    term = jnp.dot(x_ref[...], low, preferred_element_type=jnp.float32)

    @pl.when(step == 0)
    def _():
        out_ref[...] = term + h_ref[...] if has_h else term

    @pl.when(step != 0)
    def _():
        out_ref[...] += term


def update_rows(x, w, m, layer, pieces, bases, h, old, step_size):
    count, rows = len(pieces), x.shape[0]
    height, width = pieces[0].shape
    per = height // BLOCK
    stacked = w.ndim == 3
    table = jnp.stack(bases) * per

    def where(i, t):
        return t[i // per] + i % per

    lead = (1,) if stacked else ()
    at = (lambda i, t: (layer, where(i, t), 0)) if stacked else (lambda i, t: (where(i, t), 0))
    w_spec = pl.BlockSpec(lead + (BLOCK, width), at)
    in_specs = [pl.BlockSpec((rows, BLOCK), lambda i, t: (0, where(i, t))), w_spec, w_spec]
    in_specs += [
        pl.BlockSpec((BLOCK, width), lambda i, t, j=j: (jnp.clip(i - j * per, 0, per - 1), 0)) for j in range(count)
    ]
    h_spec = pl.BlockSpec((rows, width), lambda i, t: (0, 0))
    operands = [x, w, m, *pieces]
    aliases = {}
    if h is not None:
        operands.append(h)
        in_specs.append(h_spec)
    if old is not None:
        aliases = {len(operands) + 1: 0, len(operands) + 2: 1}
        operands += list(old)
        in_specs += [pl.BlockSpec(memory_space=pl.ANY)] * 2
    steps = count * per
    size = steps * BLOCK * width
    full = jax.ShapeDtypeStruct(w.shape, jnp.float32)
    new_w, new_m, out = run(
        functools.partial(rows_kernel, count, per, step_size, h is not None, old is not None), table, operands,
        in_specs, [full, full, jax.ShapeDtypeStruct((rows, width), jnp.float32)], [w_spec, w_spec, h_spec],
        steps, (2 * rows * size, 18 * size), aliases=aliases,
    )
    return (new_w, new_m), out


def cols_kernel(count, per, step_size, has_old, *refs):
    refs = list(refs)
    refs.pop(0)
    h_ref = refs.pop(0)
    w_ref, m_ref = refs.pop(0), refs.pop(0)
    pieces = [refs.pop(0) for _ in range(count)]
    new_w_ref, new_m_ref, act_ref, low_ref = refs[has_old:]
    step = pl.program_id(0)

    @pl.when(step == 0)
    def _():
        low_ref[...] = h_ref[...].astype(jnp.bfloat16)

    new_w, new_m = updated(w_ref, m_ref, select_piece(step, per, pieces), step_size)
    new_w_ref[...] = new_w
    new_m_ref[...] = new_m
    low = new_w.reshape(new_w.shape[-2:]).astype(jnp.bfloat16)
    pre = jnp.dot(low_ref[...], low, preferred_element_type=jnp.float32)
    act_ref[...] = gelu_tanh(pre).astype(jnp.bfloat16)


def update_cols(h, w, m, layer, pieces, bases, old, step_size):
    count, rows = len(pieces), h.shape[0]
    depth, width = pieces[0].shape
    per = width // BLOCK
    table = jnp.stack(bases) * per

    def where(i, t):
        return t[i // per] + i % per

    w_spec = pl.BlockSpec((1, depth, BLOCK), lambda i, t: (layer, 0, where(i, t)))
    a_spec = pl.BlockSpec((rows, BLOCK), lambda i, t: (0, where(i, t)))
    in_specs = [pl.BlockSpec((rows, depth), lambda i, t: (0, 0)), w_spec, w_spec]
    in_specs += [
        pl.BlockSpec((depth, BLOCK), lambda i, t, j=j: (0, jnp.clip(i - j * per, 0, per - 1))) for j in range(count)
    ]
    operands = [h, w, m, *pieces]
    aliases = {}
    kept = [(out_idx, value) for out_idx, value in enumerate(old) if value is not None]
    for out_idx, value in kept:
        aliases[len(operands) + 1] = out_idx
        operands.append(value)
        in_specs.append(pl.BlockSpec(memory_space=pl.ANY))
    steps = count * per
    size = steps * BLOCK * depth
    full = jax.ShapeDtypeStruct(w.shape, jnp.float32)
    new_w, new_m, act = run(
        functools.partial(cols_kernel, count, per, step_size, len(kept)), table, operands,
        in_specs, [full, full, jax.ShapeDtypeStruct((rows, w.shape[2]), jnp.bfloat16)], [w_spec, w_spec, a_spec],
        steps, (2 * rows * size, 18 * size), [pltpu.VMEM((rows, depth), jnp.bfloat16)], aliases,
    )
    return (new_w, new_m), act


def solution(mesh):
    group_size = mesh.shape["data"]

    def device_steps(w_in, w_up, w_down, mom_in, mom_up, mom_down, x_now, y_now, x_next, y_next):
        local_rows, model_width = y_now.shape
        layer_count = w_up.shape[0]
        inner = w_up.shape[2]
        step_size = 4.0 * model_width / (inner * (layer_count + 1))
        along_x, along_y = Plan(2, 4, group_size), Plan(4, 2, group_size)
        half = x_now.shape[1] // 2

        quarters_x, quarters_y = along_x.quarters(), along_y.quarters()
        halves = quarters_x + [4 + idx for idx in quarters_y]
        x_parts = split_cols(x_now, jnp.stack(halves), half // 4)
        in_wide = [along_x.exchange_wide(x_parts[:4]), along_y.exchange_wide(x_parts[4:])]

        h_state = in_forward(x_now, w_in, jnp.stack(halves))
        saved = []
        for layer in range(layer_count):
            h_low = h_state.astype(jnp.bfloat16)
            up_near = along_y.exchange_narrow(h_low)
            pre_act, *act_parts = up_forward(h_low, w_up, layer, quarters_x)
            down_wide = along_x.exchange_wide(act_parts)
            h_state = add_product(h_state, act_parts, w_down, layer, quarters_x, False)
            saved.append((up_near, down_wide, pre_act))
        cot_state = (h_state - y_now.astype(jnp.float32)) / (local_rows * group_size * model_width)

        def share(lhs, rhs):
            lhs, rhs = jnp.concatenate(lhs), jnp.concatenate(rhs)
            value = lax.dot_general(lhs, rhs, ROW_CONTRACT, preferred_element_type=jnp.float32)
            return value.astype(jnp.bfloat16)

        factors = [None] * layer_count
        for layer in reversed(range(layer_count)):
            up_near, down_wide, pre_act = saved[layer]
            cot_low = cot_state.astype(jnp.bfloat16)
            cot_near = along_x.exchange_narrow(cot_low)
            pre_parts = down_backward(cot_low, w_down, layer, pre_act, quarters_y)
            pre_wide = along_y.exchange_wide(pre_parts)
            cot_state = add_product(cot_state, pre_parts, w_up, layer, quarters_y, True)
            factors[layer] = (down_wide, cot_near, up_near, pre_wide)
        cot_low = cot_state.astype(jnp.bfloat16)
        cot_near = [along_x.exchange_narrow(cot_low), along_y.exchange_narrow(cot_low)]

        up_sums, down_sums, in_sums = [None] * layer_count, [None] * layer_count, [None] * 2
        for layer in reversed(range(layer_count)):
            down_wide, near, up_near, pre_wide = factors[layer]
            up_sums[layer] = along_y.reduce_piece(share(up_near, pre_wide), 1)
            down_sums[layer] = along_x.reduce_piece(share(down_wide, near), 0)
        for part, plan in enumerate((along_x, along_y)):
            in_sums[part] = plan.reduce_piece(share(in_wide[part], cot_near[part]), 0)

        h_state, new_in, new_up, new_down = None, None, None, None
        groups = [plan.gather(own) for plan, own in zip((along_x, along_y), in_sums)]
        for idx in range(4):
            tagged = groups[0][idx] + [(value, base + 8) for value, base in groups[1][idx]]
            pieces, bases = zip(*tagged)
            new_in, h_state = update_rows(x_next, w_in, mom_in, 0, pieces, bases, h_state, new_in, step_size)
        for layer in range(layer_count):
            act_low = None
            for tagged in along_y.gather(up_sums[layer]):
                pieces, bases = zip(*tagged)
                old = (None, None, act_low) if new_up is None else (*new_up, act_low)
                new_up, act_low = update_cols(h_state, w_up, mom_up, layer, pieces, bases, old, step_size)
            for tagged in along_x.gather(down_sums[layer]):
                pieces, bases = zip(*tagged)
                new_down, h_state = update_rows(
                    act_low, w_down, mom_down, layer, pieces, bases, h_state, new_down, step_size
                )
        loss_next = jnp.sum(jnp.square(h_state - y_next.astype(jnp.float32)), axis=1) / (2 * model_width)
        return (new_in[0], new_up[0], new_down[0], new_in[1], new_up[1], new_down[1], loss_next, h_state)

    param_spec = P()
    row_spec = P("data", None)

    return jax.shard_map(
        device_steps,
        mesh=mesh,
        in_specs=(param_spec,) * 6 + (row_spec,) * 4,
        out_specs=(param_spec,) * 6 + (P("data"), row_spec),
        check_vma=False,
    )
```

time: 2850 us -> 2330 us (0.82)
  Pallas kernels: 0 us -> 935 us
  other arithmetic: 647 us -> 61.7 us
  matrix products: 526 us -> 120 us
  waiting for transfers between devices: 1390 us -> 1100 us
  local copies, waits for them, and re-layouts: 264 us -> 31.4 us
  starting transfers between devices: 0.08 us -> 76 us
    psum x2 -> x0, waiting for transfers between devices: 1390 us -> none  [the longest x1 903 us: device_steps(): grad_in = lax.psum(local_in.astype(jnp.bfloat16), 'data')]
    ppermute x0 -> x83, waiting for transfers between devices: none -> 1100 us  [hop(): lax.ppermute(value, 'data', [(i, i ^ mask) for i in range(self.size)])]
    pallas_call x0 -> x30, Pallas kernels: none -> 935 us  [run(): pl.pallas_call(kernel, grid_spec=pltpu.PrefetchScalarGridSpec(num_scalar_...]
    convert_element_type x4 -> x11, other arithmetic: 550 us -> 50.3 us  [the longest x6 28.9 us: reduce_piece(): (keep.astype(jnp.float32) + other.astype(jnp.float32)).astype(jnp.bfloat16)]
    dot_general x19 -> x6, matrix products: 526 us -> 120 us  [share(): lax.dot_general(lhs, rhs, ROW_CONTRACT, preferred_element_type=jnp.float32)]
    unnamed x18 -> x50, local copies, waits for them, and re-layouts: 264 us -> 6.77 us
    sub x1 -> x0, other arithmetic: 95.6 us -> none  [device_steps(): new_w_in = w_in - step_size * new_mom_in]
    ppermute x0 -> x83, starting transfers between devices: none -> 76 us  [hop(): lax.ppermute(value, 'data', [(i, i ^ mask) for i in range(self.size)])]
  transfers between devices with their start and end apart: 2 -> 83, of which waited for: 2 -> 23; matrix products, arithmetic and copies ran while one was open for 17% -> 8% of each run, Pallas kernels for 0% -> 27%
where the time goes in v1:
time: 2330 us; the launch traced here: 2320 us
  waiting for transfers between devices  1100 us (47%)
  Pallas kernels  935 us (40%)
  matrix products  120 us (5%)
  starting transfers between devices  76 us (3%)
  other arithmetic  61.7 us (3%)
  local copies, waits for them, and re-layouts  31.4 us (1%)
    ppermute x83, waiting for transfers between devices, hop(): lax.ppermute(value, 'data', [(i, i ^ mask) for i in range(self.size)])  1100 us
    pallas_call x30, Pallas kernels, run(): pl.pallas_call(kernel, grid_spec=pltpu.PrefetchScalarGridSpec(num_scalar_...  935 us
    dot_general x6, matrix products, share(): lax.dot_general(lhs, rhs, ROW_CONTRACT, preferred_element_type=jnp.float32)  120 us
    ppermute x83, starting transfers between devices, hop(): lax.ppermute(value, 'data', [(i, i ^ mask) for i in range(self.size)])  76 us
  transfers between devices with their start and end apart: 83, of which 23 were waited for; matrix products, arithmetic and copies ran while one was open for 8% of the time, Pallas kernels for 27%

profile of v1, /device:TPU:1, one launch (start us, length us, event | category | flops | bytes accessed | tf_op | source)
XLA Modules:
  0.0 2323.3 jit_solution(4572275972477038334)
XLA Ops:
  37.6 37.5 %shard_map.163 = (f32[512,8192]{1,0:T(8,128)}, bf16[512,2048]{1,0:T(8,128)(2,1)}, bf16[512,2048]{1,0:T(8,128)(2,1)}, bf16[512,2048]{1,0:T(8,128)(2,1)}, bf16[512,2048]{1,0:T(8,128)(2,1)}) custom-call(s32[4]{0:T(128)} %get-tuple-element.183.table_ref, bf16[512,2048]{1,0:T(8,128)(2,1)} %convert_element_type.93.p_ref, f32[2,2048,8192]{2,1,0:T(8,128)} %refs_2_.35), custom_call_target="tpu_custom_call" | custom-call | flops 17179869184 | bytes 92274688 | tf_op jit(solution)/shard_map/pallas_call | solution.py:75
  75.1 32.7 %shard_map.164.base_ref = f32[512,2048]{1,0:T(8,128)} custom-call(s32[4]{0:T(128)} %get-tuple-element.183.table_ref, f32[512,2048]{1,0:T(8,128)} %shard_map.162.base_ref, f32[2,8192,2048]{2,1,0:T(8,128)} %refs_2_.39, bf16[512,2048]{1,0:T(8,128)(2,1)} %get-tuple-element.98.refs_0_, bf16[512,2048]{1,0:T(8,128)(2,1)} %get-tuple-element.99.refs_1_, ...), custom_call_target="tpu_custom_call" | custom-call | flops 17179869184 | bytes 75497472 | tf_op jit(solution)/shard_map/pallas_call | solution.py:75
  111.7 37.5 %shard_map.165 = (f32[512,8192]{1,0:T(8,128)}, bf16[512,2048]{1,0:T(8,128)(2,1)}, bf16[512,2048]{1,0:T(8,128)(2,1)}, bf16[512,2048]{1,0:T(8,128)(2,1)}, bf16[512,2048]{1,0:T(8,128)(2,1)}) custom-call(s32[4]{0:T(128)} %get-tuple-element.183.table_ref, bf16[512,2048]{1,0:T(8,128)(2,1)} %convert_element_type.94.p_ref, f32[2,2048,8192]{2,1,0:T(8,128)} %refs_2_.35), custom_call_target="tpu_custom_call" | custom-call | flops 17179869184 | bytes 92274688 | tf_op jit(solution)/shard_map/pallas_call | solution.py:75
  149.2 33.3 %shard_map.166 = f32[512,2048]{1,0:T(8,128)} custom-call(s32[4]{0:T(128)} %get-tuple-element.183.table_ref, f32[512,2048]{1,0:T(8,128)} %shard_map.164.base_ref, f32[2,8192,2048]{2,1,0:T(8,128)} %refs_2_.39, bf16[512,2048]{1,0:T(8,128)(2,1)} %get-tuple-element.102.refs_0_, bf16[512,2048]{1,0:T(8,128)(2,1)} %get-tuple-element.103.refs_1_, ...), custom_call_target="tpu_custom_call" | custom-call | flops 17179869184 | bytes 75497472 | tf_op jit(solution)/shard_map/pallas_call | solution.py:75
  188.5 38.0 %shard_map.167 = (bf16[512,2048]{1,0:T(8,128)(2,1)}, bf16[512,2048]{1,0:T(8,128)(2,1)}, bf16[512,2048]{1,0:T(8,128)(2,1)}, bf16[512,2048]{1,0:T(8,128)(2,1)}) custom-call(s32[4]{0:T(128)} %get-tuple-element.182.table_ref, bf16[512,2048]{1,0:T(8,128)(2,1)} %get-tuple-element.180.c_ref, f32[2,8192,2048]{2,1,0:T(8,128)} %refs_2_.39, ...), custom_call_target="tpu_custom_call" | custom-call | flops 17179869184 | bytes 92274688 | tf_op jit(solution)/shard_map/pallas_call | solution.py:75
  226.5 33.0 %shard_map.168.base_ref = f32[512,2048]{1,0:T(8,128)} custom-call(s32[4]{0:T(128)} %get-tuple-element.182.table_ref, f32[512,2048]{1,0:T(8,128)} %get-tuple-element.181.base_ref, f32[2,2048,8192]{2,1,0:T(8,128)} %refs_2_.35, bf16[512,2048]{1,0:T(8,128)(2,1)} %get-tuple-element.107.refs_0_, bf16[512,2048]{1,0:T(8,128)(2,1)} %get-tuple-element.108.refs_1_, ...), custom_call_target="tpu_custom_call" | custom-call | flops 17179869184 | bytes 75497472 | tf_op jit(solution)/shard_map/pallas_call | solution.py:75
  263.4 38.2 %shard_map.169 = (bf16[512,2048]{1,0:T(8,128)(2,1)}, bf16[512,2048]{1,0:T(8,128)(2,1)}, bf16[512,2048]{1,0:T(8,128)(2,1)}, bf16[512,2048]{1,0:T(8,128)(2,1)}) custom-call(s32[4]{0:T(128)} %get-tuple-element.182.table_ref, bf16[512,2048]{1,0:T(8,128)(2,1)} %convert_element_type.97.c_ref, f32[2,8192,2048]{2,1,0:T(8,128)} %refs_2_.39, ...), custom_call_target="tpu_custom_call" | custom-call | flops 17179869184 | bytes 92274688 | tf_op jit(solution)/shard_map/pallas_call | solution.py:75
  315.2 33.1 %shard_map.170 = f32[512,2048]{1,0:T(8,128)} custom-call(s32[4]{0:T(128)} %get-tuple-element.182.table_ref, f32[512,2048]{1,0:T(8,128)} %shard_map.168.base_ref, f32[2,2048,8192]{2,1,0:T(8,128)} %refs_2_.35, bf16[512,2048]{1,0:T(8,128)(2,1)} %get-tuple-element.112.refs_0_, bf16[512,2048]{1,0:T(8,128)(2,1)} %get-tuple-element.113.refs_1_, ...), custom_call_target="tpu_custom_call" | custom-call | flops 17179869184 | bytes 75497472 | tf_op jit(solution)/shard_map/pallas_call | solution.py:75
  413.2 37.0 %collective-permute-done.13 = bf16[512,2048]{1,0:T(8,128)(2,1)} collective-permute-done((bf16[512,2048]{1,0:T(8,128)(2,1)}, bf16[512,2048]{1,0:T(8,128)(2,1)}, u32[]{:S(2)}, u32[]{:S(2)}) %collective-permute-start.13) | collective-permute-done | bytes 2097184 | tf_op jit(solution)/shard_map/ppermute | solution.py:43
  451.9 44.2 %collective-permute-done.32 = bf16[512,2048]{1,0:T(8,128)(2,1)} collective-permute-done((bf16[512,2048]{1,0:T(8,128)(2,1)}, bf16[512,2048]{1,0:T(8,128)(2,1)}, u32[]{:S(2)}, u32[]{:S(2)}) %collective-permute-start.32) | collective-permute-done | bytes 2097184 | tf_op jit(solution)/shard_map/ppermute | solution.py:43
  496.4 43.7 %collective-permute-done.28 = bf16[512,2048]{1,0:T(8,128)(2,1)} collective-permute-done((bf16[512,2048]{1,0:T(8,128)(2,1)}, bf16[512,2048]{1,0:T(8,128)(2,1)}, u32[]{:S(2)}, u32[]{:S(2)}) %collective-permute-start.28) | collective-permute-done | bytes 2097184 | tf_op jit(solution)/shard_map/ppermute | solution.py:43
  636.0 41.7 %collective-permute-done.43 = bf16[512,2048]{1,0:T(8,128)(2,1)} collective-permute-done((bf16[512,2048]{1,0:T(8,128)(2,1)}, bf16[512,2048]{1,0:T(8,128)(2,1)}, u32[]{:S(2)}, u32[]{:S(2)}) %collective-permute-start.43) | collective-permute-done | bytes 2097184 | tf_op jit(solution)/shard_map/ppermute | solution.py:43
  820.5 93.3 %collective-permute-done.70 = bf16[512,2048]{1,0:T(8,128)(2,1)} collective-permute-done((bf16[512,2048]{1,0:T(8,128)(2,1)}, bf16[512,2048]{1,0:T(8,128)(2,1)}, u32[]{:S(2)}, u32[]{:S(2)}) %collective-permute-start.70) | collective-permute-done | bytes 2097184 | tf_op jit(solution)/shard_map/ppermute | solution.py:43
  915.1 45.4 %collective-permute-done.71 = bf16[512,2048]{1,0:T(8,128)(2,1)} collective-permute-done((bf16[512,2048]{1,0:T(8,128)(2,1)}, bf16[512,2048]{1,0:T(8,128)(2,1)}, u32[]{:S(2)}, u32[]{:S(2)}) %collective-permute-start.71) | collective-permute-done | bytes 2097184 | tf_op jit(solution)/shard_map/ppermute | solution.py:43
  991.9 105.6 %collective-permute-done.16.refs_6_ = bf16[512,2048]{1,0:T(8,128)(2,1)} collective-permute-done((bf16[512,2048]{1,0:T(8,128)(2,1)S(1)}, bf16[512,2048]{1,0:T(8,128)(2,1)}, u32[]{:S(2)}, u32[]{:S(2)}) %collective-permute-start.16) | collective-permute-done | bytes 2097184 | tf_op jit(solution)/shard_map/ppermute | solution.py:43
  1099.7 45.7 %collective-permute-done.20.refs_5_ = bf16[512,2048]{1,0:T(8,128)(2,1)} collective-permute-done((bf16[512,2048]{1,0:T(8,128)(2,1)}, bf16[512,2048]{1,0:T(8,128)(2,1)}, u32[]{:S(2)}, u32[]{:S(2)}) %collective-permute-start.20) | collective-permute-done | bytes 2097184 | tf_op jit(solution)/shard_map/ppermute | solution.py:43
  1145.8 36.4 %collective-permute-done.7.refs_4_ = bf16[512,2048]{1,0:T(8,128)(2,1)} collective-permute-done((bf16[512,2048]{1,0:T(8,128)(2,1)}, bf16[512,2048]{1,0:T(8,128)(2,1)}, u32[]{:S(2)}, u32[]{:S(2)}) %collective-permute-start.7) | collective-permute-done | bytes 2097184 | tf_op jit(solution)/shard_map/ppermute | solution.py:43
  1203.8 38.2 %collective-permute-done.17.refs_6_ = bf16[512,2048]{1,0:T(8,128)(2,1)} collective-permute-done((bf16[512,2048]{1,0:T(8,128)(2,1)}, bf16[512,2048]{1,0:T(8,128)(2,1)}, u32[]{:S(2)}, u32[]{:S(2)}) %collective-permute-start.17) | collective-permute-done | bytes 2097184 | tf_op jit(solution)/shard_map/ppermute | solution.py:43
  1251.4 81.5 %collective-permute-done.34.refs_4_ = bf16[2048,1024]{1,0:T(8,128)(2,1)} collective-permute-done((bf16[2048,1024]{1,0:T(8,128)(2,1)}, bf16[2048,1024]{1,0:T(8,128)(2,1)}, u32[]{:S(2)}, u32[]{:S(2)}) %collective-permute-start.34) | collective-permute-done | bytes 4194336 | tf_op jit(solution)/shard_map/ppermute | solution.py:43
  1342.3 79.6 %collective-permute-done.48.refs_4_ = bf16[1024,2048]{1,0:T(8,128)(2,1)} collective-permute-done((bf16[1024,2048]{1,0:T(8,128)(2,1)S(1)}, bf16[1024,2048]{1,0:T(8,128)(2,1)}, u32[]{:S(2)}, u32[]{:S(2)}) %collective-permute-start.48) | collective-permute-done | bytes 4194336 | tf_op jit(solution)/shard_map/ppermute | solution.py:43
  1426.2 86.5 %collective-permute-done.62.refs_4_ = bf16[2048,1024]{1,0:T(8,128)(2,1)} collective-permute-done((bf16[2048,1024]{1,0:T(8,128)(2,1)S(1)}, bf16[2048,1024]{1,0:T(8,128)(2,1)}, u32[]{:S(2)}, u32[]{:S(2)}) %collective-permute-start.62) | collective-permute-done | bytes 4194336 | tf_op jit(solution)/shard_map/ppermute | solution.py:43
  1515.5 86.1 %collective-permute-done.76.refs_4_ = bf16[1024,2048]{1,0:T(8,128)(2,1)} collective-permute-done((bf16[1024,2048]{1,0:T(8,128)(2,1)S(1)}, bf16[1024,2048]{1,0:T(8,128)(2,1)}, u32[]{:S(2)}, u32[]{:S(2)}) %collective-permute-start.76) | collective-permute-done | bytes 4194336 | tf_op jit(solution)/shard_map/ppermute | solution.py:43
  1607.9 88.3 %collective-permute-done.35.refs_4_ = bf16[2048,1024]{1,0:T(8,128)(2,1)} collective-permute-done((bf16[2048,1024]{1,0:T(8,128)(2,1)}, bf16[2048,1024]{1,0:T(8,128)(2,1)}, u32[]{:S(2)}, u32[]{:S(2)}) %collective-permute-start.35) | collective-permute-done | bytes 4194336 | tf_op jit(solution)/shard_map/ppermute | solution.py:43
  1738.0 32.5 %shard_map.172 = (f32[8192,2048]{1,0:T(8,128)}, f32[8192,2048]{1,0:T(8,128)}, f32[512,2048]{1,0:T(8,128)}) custom-call(s32[4]{0:T(128)} %add_multiply_fusion.2.refs_0_, bf16[512,8192]{1,0:T(8,128)(2,1)} %refs_1_.7, f32[8192,2048]{1,0:T(8,128)} %refs_2_.23, f32[8192,2048]{1,0:T(8,128)} %refs_3_.23, ...), custom_call_target="tpu_custom_call", output_to_operand_aliasing={{0}: (9, {}), {1}: (10, {})} | custom-call | flops 4294967296 | bytes 75497472 | tf_op jit(solution)/shard_map/pallas_call | solution.py:75
  (262 shorter events, 1052.5 us)
Async XLA Ops:
  777.7 184.3 %collective-permute-start.33 = (bf16[2048,1024]{1,0:T(8,128)(2,1)}, bf16[2048,1024]{1,0:T(8,128)(2,1)}, u32[]{:S(2)}, u32[]{:S(2)}) collective-permute-start(bf16[2048,1024]{1,0:T(8,128)(2,1)} %constant_dynamic-slice_fusion.3), channel_id=1, source_target_pairs={{0,2},{1,3},{2,0},{3,1},{4,6},{5,7},{6,4},{7,5}} | collective-permute-start | bytes 12582920 | tf_op jit(solution)/shard_map/ppermute | solution.py:43
  781.6 178.9 %collective-permute-start.71 = (bf16[512,2048]{1,0:T(8,128)(2,1)}, bf16[512,2048]{1,0:T(8,128)(2,1)}, u32[]{:S(2)}, u32[]{:S(2)}) collective-permute-start(bf16[512,2048]{1,0:T(8,128)(2,1)} %get-tuple-element.103.refs_1_), channel_id=1, source_target_pairs={{0,3},{1,2},{2,1},{3,0},{4,7},{5,6},{6,5},{7,4}} | collective-permute-start | bytes 6291464 | tf_op jit(solution)/shard_map/ppermute | solution.py:43
  783.4 177.2 %collective-permute-start.74 = (bf16[512,2048]{1,0:T(8,128)(2,1)}, bf16[512,2048]{1,0:T(8,128)(2,1)}, u32[]{:S(2)}, u32[]{:S(2)}) collective-permute-start(bf16[512,2048]{1,0:T(8,128)(2,1)} %collective-permute-done.73), channel_id=1, source_target_pairs={{0,1},{1,0},{2,3},{3,2},{4,5},{5,4},{6,7},{7,6}} | collective-permute-start | bytes 6291464 | tf_op jit(solution)/shard_map/ppermute | solution.py:43
  783.4 179.8 %collective-permute-start.26 = (bf16[512,2048]{1,0:T(8,128)(2,1)S(1)}, bf16[512,2048]{1,0:T(8,128)(2,1)}, u32[]{:S(2)}, u32[]{:S(2)}) collective-permute-start(bf16[512,2048]{1,0:T(8,128)(2,1)S(1)} %add_convert_fusion.4.refs_6_), channel_id=1, source_target_pairs={{0,1},{1,0},{2,3},{3,2},{4,5},{5,4},{6,7},{7,6}} | collective-permute-start | bytes 6291464 | tf_op jit(solution)/shard_map/ppermute | solution.py:43
  913.8 273.1 %collective-permute-start.47 = (bf16[1024,2048]{1,0:T(8,128)(2,1)}, bf16[1024,2048]{1,0:T(8,128)(2,1)}, u32[]{:S(2)}, u32[]{:S(2)}) collective-permute-start(bf16[1024,2048]{1,0:T(8,128)(2,1)} %constant_dynamic-slice_fusion.2), channel_id=1, source_target_pairs={{0,4},{1,5},{2,6},{3,7},{4,0},{5,1},{6,2},{7,3}} | collective-permute-start | bytes 12582920 | tf_op jit(solution)/shard_map/ppermute | solution.py:43
  960.5 226.4 %collective-permute-start.61 = (bf16[2048,1024]{1,0:T(8,128)(2,1)}, bf16[2048,1024]{1,0:T(8,128)(2,1)}, u32[]{:S(2)}, u32[]{:S(2)}) collective-permute-start(bf16[2048,1024]{1,0:T(8,128)(2,1)} %constant_dynamic-slice_fusion.1), channel_id=1, source_target_pairs={{0,2},{1,3},{2,0},{3,1},{4,6},{5,7},{6,4},{7,5}} | collective-permute-start | bytes 12582920 | tf_op jit(solution)/shard_map/ppermute | solution.py:43
  991.7 203.3 %collective-permute-start.75 = (bf16[1024,2048]{1,0:T(8,128)(2,1)}, bf16[1024,2048]{1,0:T(8,128)(2,1)}, u32[]{:S(2)}, u32[]{:S(2)}) collective-permute-start(bf16[1024,2048]{1,0:T(8,128)(2,1)} %constant_dynamic-slice_fusion), channel_id=1, source_target_pairs={{0,4},{1,5},{2,6},{3,7},{4,0},{5,1},{6,2},{7,3}} | collective-permute-start | bytes 12582920 | tf_op jit(solution)/shard_map/ppermute | solution.py:43
  1244.3 177.5 %collective-permute-start.48 = (bf16[1024,2048]{1,0:T(8,128)(2,1)S(1)}, bf16[1024,2048]{1,0:T(8,128)(2,1)}, u32[]{:S(2)}, u32[]{:S(2)}) collective-permute-start(bf16[1024,2048]{1,0:T(8,128)(2,1)S(1)} %add_convert_fusion.2.refs_4_), channel_id=1, source_target_pairs={{0,4},{1,5},{2,6},{3,7},{4,0},{5,1},{6,2},{7,3}} | collective-permute-start | bytes 12582920 | tf_op jit(solution)/shard_map/ppermute | solution.py:43
  1245.6 177.5 %collective-permute-start.52 = (bf16[1024,2048]{1,0:T(8,128)(2,1)S(1)}, bf16[1024,2048]{1,0:T(8,128)(2,1)}, u32[]{:S(2)}, u32[]{:S(2)}) collective-permute-start(bf16[1024,2048]{1,0:T(8,128)(2,1)S(1)} %add_convert_fusion.2.refs_4_), channel_id=1, source_target_pairs={{0,2},{1,3},{2,0},{3,1},{4,6},{5,7},{6,4},{7,5}} | collective-permute-start | bytes 12582920 | tf_op jit(solution)/shard_map/ppermute | solution.py:43
  1335.7 176.9 %collective-permute-start.62 = (bf16[2048,1024]{1,0:T(8,128)(2,1)S(1)}, bf16[2048,1024]{1,0:T(8,128)(2,1)}, u32[]{:S(2)}, u32[]{:S(2)}) collective-permute-start(bf16[2048,1024]{1,0:T(8,128)(2,1)S(1)} %add_convert_fusion.1.refs_4_), channel_id=1, source_target_pairs={{0,2},{1,3},{2,0},{3,1},{4,6},{5,7},{6,4},{7,5}} | collective-permute-start | bytes 12582920 | tf_op jit(solution)/shard_map/ppermute | solution.py:43
  1338.1 177.4 %collective-permute-start.66 = (bf16[2048,1024]{1,0:T(8,128)(2,1)S(1)}, bf16[2048,1024]{1,0:T(8,128)(2,1)}, u32[]{:S(2)}, u32[]{:S(2)}) collective-permute-start(bf16[2048,1024]{1,0:T(8,128)(2,1)S(1)} %add_convert_fusion.1.refs_4_), channel_id=1, source_target_pairs={{0,4},{1,5},{2,6},{3,7},{4,0},{5,1},{6,2},{7,3}} | collective-permute-start | bytes 12582920 | tf_op jit(solution)/shard_map/ppermute | solution.py:43
  1421.8 179.8 %collective-permute-start.76 = (bf16[1024,2048]{1,0:T(8,128)(2,1)S(1)}, bf16[1024,2048]{1,0:T(8,128)(2,1)}, u32[]{:S(2)}, u32[]{:S(2)}) collective-permute-start(bf16[1024,2048]{1,0:T(8,128)(2,1)S(1)} %add_convert_fusion.refs_4_), channel_id=1, source_target_pairs={{0,4},{1,5},{2,6},{3,7},{4,0},{5,1},{6,2},{7,3}} | collective-permute-start | bytes 12582920 | tf_op jit(solution)/shard_map/ppermute | solution.py:43
  1423.1 179.9 %collective-permute-start.80 = (bf16[1024,2048]{1,0:T(8,128)(2,1)S(1)}, bf16[1024,2048]{1,0:T(8,128)(2,1)S(1)}, u32[]{:S(2)}, u32[]{:S(2)}) collective-permute-start(bf16[1024,2048]{1,0:T(8,128)(2,1)S(1)} %add_convert_fusion.refs_4_), channel_id=1, source_target_pairs={{0,2},{1,3},{2,0},{3,1},{4,6},{5,7},{6,4},{7,5}} | collective-permute-start | bytes 12582920 | tf_op jit(solution)/shard_map/ppermute | solution.py:43
  1423.3 184.1 %collective-permute-start.37 = (bf16[2048,1024]{1,0:T(8,128)(2,1)}, bf16[2048,1024]{1,0:T(8,128)(2,1)}, u32[]{:S(2)}, u32[]{:S(2)}) collective-permute-start(bf16[2048,1024]{1,0:T(8,128)(2,1)} %collective-permute-done.34.refs_4_), channel_id=1, source_target_pairs={{0,1},{1,0},{2,3},{3,2},{4,5},{5,4},{6,7},{7,6}} | collective-permute-start | bytes 12582920 | tf_op jit(solution)/shard_map/ppermute | solution.py:43
  1696.3 139.1 %collective-permute-start.63 = (bf16[2048,1024]{1,0:T(8,128)(2,1)}, bf16[2048,1024]{1,0:T(8,128)(2,1)}, u32[]{:S(2)}, u32[]{:S(2)}) collective-permute-start(bf16[2048,1024]{1,0:T(8,128)(2,1)} %collective-permute-done.62.refs_4_), channel_id=1, source_target_pairs={{0,4},{1,5},{2,6},{3,7},{4,0},{5,1},{6,2},{7,3}} | collective-permute-start | bytes 12582920 | tf_op jit(solution)/shard_map/ppermute | solution.py:43
  1698.5 165.5 %collective-permute-start.67 = (bf16[2048,1024]{1,0:T(8,128)(2,1)}, bf16[2048,1024]{1,0:T(8,128)(2,1)}, u32[]{:S(2)}, u32[]{:S(2)}) collective-permute-start(bf16[2048,1024]{1,0:T(8,128)(2,1)} %collective-permute-done.66.refs_5_), channel_id=1, source_target_pairs={{0,1},{1,0},{2,3},{3,2},{4,5},{5,4},{6,7},{7,6}} | collective-permute-start | bytes 12582920 | tf_op jit(solution)/shard_map/ppermute | solution.py:43
  1699.7 220.4 %collective-permute-start.77 = (bf16[1024,2048]{1,0:T(8,128)(2,1)}, bf16[1024,2048]{1,0:T(8,128)(2,1)}, u32[]{:S(2)}, u32[]{:S(2)}) collective-permute-start(bf16[1024,2048]{1,0:T(8,128)(2,1)} %collective-permute-done.76.refs_4_), channel_id=1, source_target_pairs={{0,2},{1,3},{2,0},{3,1},{4,6},{5,7},{6,4},{7,5}} | collective-permute-start | bytes 12582920 | tf_op jit(solution)/shard_map/ppermute | solution.py:43
  1700.0 220.6 %collective-permute-start.36 = (bf16[2048,1024]{1,0:T(8,128)(2,1)}, bf16[2048,1024]{1,0:T(8,128)(2,1)}, u32[]{:S(2)}, u32[]{:S(2)}) collective-permute-start(bf16[2048,1024]{1,0:T(8,128)(2,1)} %collective-permute-done.35.refs_4_), channel_id=1, source_target_pairs={{0,1},{1,0},{2,3},{3,2},{4,5},{5,4},{6,7},{7,6}} | collective-permute-start | bytes 12582920 | tf_op jit(solution)/shard_map/ppermute | solution.py:43
  1702.5 246.2 %collective-permute-start.50 = (bf16[1024,2048]{1,0:T(8,128)(2,1)}, bf16[1024,2048]{1,0:T(8,128)(2,1)}, u32[]{:S(2)}, u32[]{:S(2)}) collective-permute-start(bf16[1024,2048]{1,0:T(8,128)(2,1)} %collective-permute-done.49.refs_4_), channel_id=1, source_target_pairs={{0,1},{1,0},{2,3},{3,2},{4,5},{5,4},{6,7},{7,6}} | collective-permute-start | bytes 12582920 | tf_op jit(solution)/shard_map/ppermute | solution.py:43
  1835.4 326.7 %collective-permute-start.64 = (bf16[2048,1024]{1,0:T(8,128)(2,1)}, bf16[2048,1024]{1,0:T(8,128)(2,1)}, u32[]{:S(2)}, u32[]{:S(2)}) collective-permute-start(bf16[2048,1024]{1,0:T(8,128)(2,1)} %collective-permute-done.63.refs_4_), channel_id=1, source_target_pairs={{0,1},{1,0},{2,3},{3,2},{4,5},{5,4},{6,7},{7,6}} | collective-permute-start | bytes 12582920 | tf_op jit(solution)/shard_map/ppermute | solution.py:43
  1864.0 326.2 %collective-permute-start.82 = (bf16[1024,2048]{1,0:T(8,128)(2,1)}, bf16[1024,2048]{1,0:T(8,128)(2,1)}, u32[]{:S(2)}, u32[]{:S(2)}) collective-permute-start(bf16[1024,2048]{1,0:T(8,128)(2,1)} %copy-done), channel_id=1, source_target_pairs={{0,1},{1,0},{2,3},{3,2},{4,5},{5,4},{6,7},{7,6}} | collective-permute-start | bytes 12582920 | tf_op jit(solution)/shard_map/ppermute | solution.py:43
  1920.1 334.7 %collective-permute-start.79 = (bf16[1024,2048]{1,0:T(8,128)(2,1)}, bf16[1024,2048]{1,0:T(8,128)(2,1)}, u32[]{:S(2)}, u32[]{:S(2)}) collective-permute-start(bf16[1024,2048]{1,0:T(8,128)(2,1)} %collective-permute-done.76.refs_4_), channel_id=1, source_target_pairs={{0,1},{1,0},{2,3},{3,2},{4,5},{5,4},{6,7},{7,6}} | collective-permute-start | bytes 12582920 | tf_op jit(solution)/shard_map/ppermute | solution.py:43
  1920.6 334.2 %collective-permute-start.81 = (bf16[1024,2048]{1,0:T(8,128)(2,1)}, bf16[1024,2048]{1,0:T(8,128)(2,1)}, u32[]{:S(2)}, u32[]{:S(2)}) collective-permute-start(bf16[1024,2048]{1,0:T(8,128)(2,1)} %copy-done.6), channel_id=1, source_target_pairs={{0,1},{1,0},{2,3},{3,2},{4,5},{5,4},{6,7},{7,6}} | collective-permute-start | bytes 12582920 | tf_op jit(solution)/shard_map/ppermute | solution.py:43
  1948.7 338.4 %collective-permute-start.78 = (bf16[1024,2048]{1,0:T(8,128)(2,1)}, bf16[1024,2048]{1,0:T(8,128)(2,1)}, u32[]{:S(2)}, u32[]{:S(2)}) collective-permute-start(bf16[1024,2048]{1,0:T(8,128)(2,1)} %collective-permute-done.77.refs_4_), channel_id=1, source_target_pairs={{0,1},{1,0},{2,3},{3,2},{4,5},{5,4},{6,7},{7,6}} | collective-permute-start | bytes 12582920 | tf_op jit(solution)/shard_map/ppermute | solution.py:43
  (84 other events, 5668.1 us)

commit v2 on v1

--- a/solution.py
+++ b/solution.py
@@ -10,8 +10,8 @@
 
 MOMENTUM = 0.9
 BLOCK = 256
-STEP_BLOCK = 1024
 CHUNK = 256
+UPDATE_ORDER = ((1, 0), (0, 0), (1, 1), (0, 1), (1, 2), (0, 2), (1, 3), (0, 3))
 ROW_CONTRACT = (((0,), (0,)), ((), ()))
 COL_CONTRACT = (((1,), (1,)), ((), ()))
 
@@ -24,20 +24,20 @@
     def __init__(self, first, second, size):
         self.first, self.second, self.size = first, second, size
         me = lax.axis_index("data")
-        bit = lambda mask: (me // mask) % 2
-        self.f, self.s, self.c = bit(first), bit(second), bit(1)
-
-    def quarter(self, flip_f, flip_c):
-        f = 1 - self.f if flip_f else self.f
-        c = 1 - self.c if flip_c else self.c
-        return 2 * f + c
+        self.s = (me // second) % 2
+        self.bits = {mask: (me // mask) % 2 for mask in (1, 2, 4)}
 
     def piece(self, flip_f, flip_s, flip_c):
-        s = 1 - self.s if flip_s else self.s
-        return 2 * self.quarter(flip_f, flip_c) + s
-
-    def quarters(self):
-        return [self.quarter(1, 0), self.quarter(1, 1), self.quarter(0, 1), self.quarter(0, 0)]
+        flips = {self.first: flip_f, self.second: flip_s, 1: flip_c}
+        c, x, y = (1 - self.bits[mask] if flips[mask] else self.bits[mask] for mask in (1, 2, 4))
+        return 4 * c + 2 * x + y
+
+    def eighths(self):
+        pairs = []
+        for flip_f, flip_c in ((1, 0), (1, 1), (0, 1), (0, 0)):
+            ours, other = self.piece(flip_f, 0, flip_c), self.piece(flip_f, 1, flip_c)
+            pairs += [jnp.where(self.s == 0, ours, other), jnp.where(self.s == 0, other, ours)]
+        return pairs
 
     def hop(self, value, mask):
         return lax.ppermute(value, "data", [(i, i ^ mask) for i in range(self.size)])
@@ -84,10 +84,6 @@
     )(table, *operands)
 
 
-def lower(ref):
-    return ref[...].reshape(ref.shape[-2:]).astype(jnp.bfloat16)
-
-
 def store_part(step, per, part_refs, value):
     for idx, ref in enumerate(part_refs):
 
@@ -108,24 +104,23 @@
 
 
 def split_kernel(table_ref, x_ref, *out_refs):
-    store_part(pl.program_id(0), 1, out_refs, x_ref[...])
-
-
-def split_cols(x, table, width):
-    rows, count = x.shape[0], table.shape[0]
-    shape = (rows, width)
+    store_part(pl.program_id(0), 2, out_refs, x_ref[...])
+
+
+def split_cols(x, table, count):
+    rows, size = x.shape[0], x.shape[1] // (2 * count)
     return run(
         split_kernel, table, [x],
-        [pl.BlockSpec(shape, lambda i, t: (0, t[i]))],
-        [jax.ShapeDtypeStruct(shape, x.dtype)] * count,
-        part_specs(count, 1, shape, 1),
-        count, (0, 4 * x.size),
+        [pl.BlockSpec((rows, size), lambda i, t: (0, t[i]))],
+        [jax.ShapeDtypeStruct((rows, 2 * size), x.dtype)] * count,
+        part_specs(count, 2, (rows, size), 1),
+        2 * count, (0, 4 * x.size),
     )
 
 
 def up_kernel(per, table_ref, p_ref, w_ref, u_ref, *act_refs):
     values = []
-    for lo in range(0, STEP_BLOCK, CHUNK):
+    for lo in range(0, w_ref.shape[2], CHUNK):
         low = w_ref[0, :, lo : lo + CHUNK].astype(jnp.bfloat16)
         pre = jnp.dot(p_ref[...], low, preferred_element_type=jnp.float32)
         u_ref[:, lo : lo + CHUNK] = pre
@@ -133,18 +128,18 @@
     store_part(pl.program_id(0), per, act_refs, jnp.concatenate(values, axis=1))
 
 
-def up_forward(p, w, layer, quarters):
+def up_forward(p, w, layer, eighths):
     (rows, depth), inner = p.shape, w.shape[2]
-    per = inner // 4 // STEP_BLOCK
-    block = lambda i, t: t[i // per] * per + i % per
+    per, size = 2, inner // 8
+    block = lambda i, t: t[i]
     return run(
-        functools.partial(up_kernel, per), jnp.stack(quarters), [p, w],
+        functools.partial(up_kernel, per), jnp.stack(eighths), [p, w],
         [
             pl.BlockSpec((rows, depth), lambda i, t: (0, 0)),
-            pl.BlockSpec((1, depth, STEP_BLOCK), lambda i, t: (layer, 0, block(i, t))),
+            pl.BlockSpec((1, depth, size), lambda i, t: (layer, 0, block(i, t))),
         ],
         [jax.ShapeDtypeStruct((rows, inner), jnp.float32)] + [jax.ShapeDtypeStruct((rows, inner // 4), jnp.bfloat16)] * 4,
-        [pl.BlockSpec((rows, STEP_BLOCK), lambda i, t: (0, block(i, t)))] + part_specs(4, per, (rows, STEP_BLOCK), 1),
+        [pl.BlockSpec((rows, size), lambda i, t: (0, block(i, t)))] + part_specs(4, per, (rows, size), 1),
         4 * per, (2 * rows * depth * inner, 4 * depth * inner + 6 * rows * inner),
     )
 
@@ -155,32 +150,32 @@
 
 def back_kernel(per, table_ref, c_ref, w_ref, u_ref, *q_refs):
     values = []
-    for lo in range(0, STEP_BLOCK, CHUNK):
+    for lo in range(0, w_ref.shape[1], CHUNK):
         act_cot = dot_nt(c_ref[...], w_ref[0, lo : lo + CHUNK, :].astype(jnp.bfloat16))
         gelu_back = jax.vjp(gelu_tanh, u_ref[:, lo : lo + CHUNK])[1]
         values.append(gelu_back(act_cot)[0].astype(jnp.bfloat16))
     store_part(pl.program_id(0), per, q_refs, jnp.concatenate(values, axis=1))
 
 
-def down_backward(c, w, layer, u, quarters):
+def down_backward(c, w, layer, u, eighths):
     (rows, width), inner = c.shape, w.shape[1]
-    per = inner // 4 // STEP_BLOCK
-    block = lambda i, t: t[i // per] * per + i % per
+    per, size = 2, inner // 8
+    block = lambda i, t: t[i]
     return run(
-        functools.partial(back_kernel, per), jnp.stack(quarters), [c, w, u],
+        functools.partial(back_kernel, per), jnp.stack(eighths), [c, w, u],
         [
             pl.BlockSpec((rows, width), lambda i, t: (0, 0)),
-            pl.BlockSpec((1, STEP_BLOCK, width), lambda i, t: (layer, block(i, t), 0)),
-            pl.BlockSpec((rows, STEP_BLOCK), lambda i, t: (0, block(i, t))),
+            pl.BlockSpec((1, size, width), lambda i, t: (layer, block(i, t), 0)),
+            pl.BlockSpec((rows, size), lambda i, t: (0, block(i, t))),
         ],
         [jax.ShapeDtypeStruct((rows, inner // 4), jnp.bfloat16)] * 4,
-        part_specs(4, per, (rows, STEP_BLOCK), 1),
+        part_specs(4, per, (rows, size), 1),
         4 * per, (2 * rows * width * inner, 4 * width * inner + 6 * rows * inner),
     )
 
 
 def add_kernel(per, transposed, table_ref, base_ref, w_ref, *refs):
-    *part_refs, out_ref = refs
+    *part_refs, out_ref, low_ref = refs
     step = pl.program_id(0)
 
     @pl.when(step == 0)
@@ -188,51 +183,60 @@
         out_ref[...] = base_ref[...]
 
     lhs = select_piece(step, per, part_refs)
-    if transposed:
-        out_ref[...] += dot_nt(lhs, lower(w_ref))
-    else:
-        out_ref[...] += jnp.dot(lhs, lower(w_ref), preferred_element_type=jnp.float32)
-
-
-def add_product(base, parts, w, layer, quarters, transposed):
+    for lo in range(0, out_ref.shape[1], 2 * CHUNK):
+        at = slice(lo, lo + 2 * CHUNK)
+        if transposed:
+            out_ref[:, at] += dot_nt(lhs, w_ref[0, at, :].astype(jnp.bfloat16))
+        else:
+            out_ref[:, at] += jnp.dot(lhs, w_ref[0, :, at].astype(jnp.bfloat16), preferred_element_type=jnp.float32)
+
+    @pl.when(step == pl.num_programs(0) - 1)
+    def _():
+        low_ref[...] = out_ref[...].astype(jnp.bfloat16)
+
+
+def add_product(base, parts, w, layer, eighths, transposed):
     rows, width = base.shape
     inner = 4 * parts[0].shape[1]
-    per = inner // 4 // STEP_BLOCK
-    block = lambda i, t: t[i // per] * per + i % per
+    per, size = 2, inner // 8
+    block = lambda i, t: t[i]
     whole = pl.BlockSpec((rows, width), lambda i, t: (0, 0))
     if transposed:
-        w_spec = pl.BlockSpec((1, width, STEP_BLOCK), lambda i, t: (layer, 0, block(i, t)))
+        w_spec = pl.BlockSpec((1, width, size), lambda i, t: (layer, 0, block(i, t)))
     else:
-        w_spec = pl.BlockSpec((1, STEP_BLOCK, width), lambda i, t: (layer, block(i, t), 0))
+        w_spec = pl.BlockSpec((1, size, width), lambda i, t: (layer, block(i, t), 0))
     return run(
-        functools.partial(add_kernel, per, transposed), jnp.stack(quarters), [base, w, *parts],
-        [whole, w_spec] + part_specs(4, per, (rows, STEP_BLOCK), 1),
-        jax.ShapeDtypeStruct((rows, width), jnp.float32),
-        whole,
+        functools.partial(add_kernel, per, transposed), jnp.stack(eighths), [base, w, *parts],
+        [whole, w_spec] + part_specs(4, per, (rows, size), 1),
+        [jax.ShapeDtypeStruct((rows, width), dtype) for dtype in (jnp.float32, jnp.bfloat16)],
+        [whole, whole],
         4 * per, (2 * rows * width * inner, 4 * width * inner + 2 * rows * inner),
     )
 
 
-def in_kernel(table_ref, x_ref, w_ref, out_ref):
-    term = jnp.dot(x_ref[...], lower(w_ref), preferred_element_type=jnp.float32)
-
+def in_kernel(table_ref, x_ref, w_ref, out_ref, low_ref):
     @pl.when(pl.program_id(0) == 0)
     def _():
-        out_ref[...] = term
-
-    @pl.when(pl.program_id(0) != 0)
-    def _():
-        out_ref[...] += term
+        out_ref[...] = jnp.zeros_like(out_ref)
+
+    for lo in range(0, out_ref.shape[1], 2 * CHUNK):
+        at = slice(lo, lo + 2 * CHUNK)
+        out_ref[:, at] += jnp.dot(x_ref[...], w_ref[:, at].astype(jnp.bfloat16), preferred_element_type=jnp.float32)
+
+    @pl.when(pl.program_id(0) == pl.num_programs(0) - 1)
+    def _():
+        low_ref[...] = out_ref[...].astype(jnp.bfloat16)
 
 
 def in_forward(x, w, table):
     (rows, depth), width = x.shape, w.shape[1]
+    size = depth // 8
     return run(
         in_kernel, table, [x, w],
-        [pl.BlockSpec((rows, STEP_BLOCK), lambda i, t: (0, i)), pl.BlockSpec((STEP_BLOCK, width), lambda i, t: (i, 0))],
-        jax.ShapeDtypeStruct((rows, width), jnp.float32),
-        pl.BlockSpec((rows, width), lambda i, t: (0, 0)),
-        depth // STEP_BLOCK, (2 * rows * depth * width, 4 * depth * width + 2 * rows * depth),
+        [pl.BlockSpec((rows, size), lambda i, t: (0, i)), pl.BlockSpec((size, width), lambda i, t: (i, 0))],
+        [jax.ShapeDtypeStruct((rows, width), dtype) for dtype in (jnp.float32, jnp.bfloat16)],
+        [pl.BlockSpec((rows, width), lambda i, t: (0, 0))] * 2,
+        depth // size, (2 * rows * depth * width, 4 * depth * width + 2 * rows * depth),
     )
 
 
@@ -260,19 +264,21 @@
         refs.pop(0), refs.pop(0)
     new_w_ref, new_m_ref, out_ref = refs
     step = pl.program_id(0)
-    new_w, new_m = updated(w_ref, m_ref, select_piece(step, per, pieces), step_size)
-    new_w_ref[...] = new_w
-    new_m_ref[...] = new_m
-    low = new_w.reshape(new_w.shape[-2:]).astype(jnp.bfloat16)
-    term = jnp.dot(x_ref[...], low, preferred_element_type=jnp.float32)
 
     @pl.when(step == 0)
     def _():
-        out_ref[...] = term + h_ref[...] if has_h else term
-
-    @pl.when(step != 0)
-    def _():
-        out_ref[...] += term
+        out_ref[...] = h_ref[...] if has_h else jnp.zeros_like(out_ref)
+
+    grad = select_piece(step, per, pieces)
+    lead = (0,) * (len(w_ref.shape) - 2)
+    for lo in range(0, out_ref.shape[1], 2 * CHUNK):
+        at = slice(lo, lo + 2 * CHUNK)
+        place = lead + (slice(None), at)
+        new_m = MOMENTUM * m_ref[place] + grad[:, at].astype(jnp.float32)
+        new_w = w_ref[place] - step_size * new_m
+        new_w_ref[place] = new_w
+        new_m_ref[place] = new_m
+        out_ref[:, at] += jnp.dot(x_ref[...], new_w.astype(jnp.bfloat16), preferred_element_type=jnp.float32)
 
 
 def update_rows(x, w, m, layer, pieces, bases, h, old, step_size):
@@ -376,21 +382,20 @@
         inner = w_up.shape[2]
         step_size = 4.0 * model_width / (inner * (layer_count + 1))
         along_x, along_y = Plan(2, 4, group_size), Plan(4, 2, group_size)
-        half = x_now.shape[1] // 2
-
-        quarters_x, quarters_y = along_x.quarters(), along_y.quarters()
-        halves = quarters_x + [4 + idx for idx in quarters_y]
-        x_parts = split_cols(x_now, jnp.stack(halves), half // 4)
+
+        halves = along_x.eighths() + [8 + idx for idx in along_y.eighths()]
+        x_parts = split_cols(x_now, jnp.stack(halves), 8)
+        up_plans, down_plans = [along_x, along_y], [along_y, along_x]
         in_wide = [along_x.exchange_wide(x_parts[:4]), along_y.exchange_wide(x_parts[4:])]
 
-        h_state = in_forward(x_now, w_in, jnp.stack(halves))
+        h_state, h_low = in_forward(x_now, w_in, jnp.stack(halves))
         saved = []
         for layer in range(layer_count):
-            h_low = h_state.astype(jnp.bfloat16)
-            up_near = along_y.exchange_narrow(h_low)
-            pre_act, *act_parts = up_forward(h_low, w_up, layer, quarters_x)
-            down_wide = along_x.exchange_wide(act_parts)
-            h_state = add_product(h_state, act_parts, w_down, layer, quarters_x, False)
+            up_plan, down_plan = up_plans[layer % 2], down_plans[layer % 2]
+            up_near = up_plan.exchange_narrow(h_low)
+            pre_act, *act_parts = up_forward(h_low, w_up, layer, down_plan.eighths())
+            down_wide = down_plan.exchange_wide(act_parts)
+            h_state, h_low = add_product(h_state, act_parts, w_down, layer, down_plan.eighths(), False)
             saved.append((up_near, down_wide, pre_act))
         cot_state = (h_state - y_now.astype(jnp.float32)) / (local_rows * group_size * model_width)
 
@@ -400,22 +405,22 @@
             return value.astype(jnp.bfloat16)
 
         factors = [None] * layer_count
+        cot_low = cot_state.astype(jnp.bfloat16)
         for layer in reversed(range(layer_count)):
+            up_plan, down_plan = up_plans[layer % 2], down_plans[layer % 2]
             up_near, down_wide, pre_act = saved[layer]
-            cot_low = cot_state.astype(jnp.bfloat16)
-            cot_near = along_x.exchange_narrow(cot_low)
-            pre_parts = down_backward(cot_low, w_down, layer, pre_act, quarters_y)
-            pre_wide = along_y.exchange_wide(pre_parts)
-            cot_state = add_product(cot_state, pre_parts, w_up, layer, quarters_y, True)
+            cot_near = down_plan.exchange_narrow(cot_low)
+            pre_parts = down_backward(cot_low, w_down, layer, pre_act, up_plan.eighths())
+            pre_wide = up_plan.exchange_wide(pre_parts)
+            cot_state, cot_low = add_product(cot_state, pre_parts, w_up, layer, up_plan.eighths(), True)
             factors[layer] = (down_wide, cot_near, up_near, pre_wide)
-        cot_low = cot_state.astype(jnp.bfloat16)
         cot_near = [along_x.exchange_narrow(cot_low), along_y.exchange_narrow(cot_low)]
 
         up_sums, down_sums, in_sums = [None] * layer_count, [None] * layer_count, [None] * 2
         for layer in reversed(range(layer_count)):
             down_wide, near, up_near, pre_wide = factors[layer]
-            up_sums[layer] = along_y.reduce_piece(share(up_near, pre_wide), 1)
-            down_sums[layer] = along_x.reduce_piece(share(down_wide, near), 0)
+            up_sums[layer] = up_plans[layer % 2].reduce_piece(share(up_near, pre_wide), 1)
+            down_sums[layer] = down_plans[layer % 2].reduce_piece(share(down_wide, near), 0)
         for part, plan in enumerate((along_x, along_y)):
             in_sums[part] = plan.reduce_piece(share(in_wide[part], cot_near[part]), 0)
 
@@ -426,16 +431,24 @@
             pieces, bases = zip(*tagged)
             new_in, h_state = update_rows(x_next, w_in, mom_in, 0, pieces, bases, h_state, new_in, step_size)
         for layer in range(layer_count):
-            act_low = None
-            for tagged in along_y.gather(up_sums[layer]):
-                pieces, bases = zip(*tagged)
+            act_low, h_up = None, h_state
+            up_groups = up_plans[layer % 2].gather(up_sums[layer])
+            down_groups = down_plans[layer % 2].gather(down_sums[layer])
+
+            def up_step(idx, new_up, act_low):
+                pieces, bases = zip(*up_groups[idx])
                 old = (None, None, act_low) if new_up is None else (*new_up, act_low)
-                new_up, act_low = update_cols(h_state, w_up, mom_up, layer, pieces, bases, old, step_size)
-            for tagged in along_x.gather(down_sums[layer]):
-                pieces, bases = zip(*tagged)
-                new_down, h_state = update_rows(
-                    act_low, w_down, mom_down, layer, pieces, bases, h_state, new_down, step_size
-                )
+                return update_cols(h_up, w_up, mom_up, layer, pieces, bases, old, step_size)
+
+            def down_step(idx, new_down, h_state, act_low):
+                pieces, bases = zip(*down_groups[idx])
+                return update_rows(act_low, w_down, mom_down, layer, pieces, bases, h_state, new_down, step_size)
+
+            for is_up, idx in UPDATE_ORDER:
+                if is_up:
+                    new_up, act_low = up_step(idx, new_up, act_low)
+                else:
+                    new_down, h_state = down_step(idx, new_down, h_state, act_low)
         loss_next = jnp.sum(jnp.square(h_state - y_next.astype(jnp.float32)), axis=1) / (2 * model_width)
         return (new_in[0], new_up[0], new_down[0], new_in[1], new_up[1], new_down[1], loss_next, h_state)
 

time: 2330 us -> 2340 us (level)
  transfers between devices with their start and end apart: 83 -> 83, of which waited for: 23 -> 30; matrix products, arithmetic and copies ran while one was open for 8% -> 8% of each run, Pallas kernels for 27% -> 38%
where the time goes in v2:
time: 2340 us; the launch traced here: 2330 us
  waiting for transfers between devices  1110 us (47%)
  Pallas kernels  923 us (39%)
  matrix products  120 us (5%)
  starting transfers between devices  98.1 us (4%)
  other arithmetic  46 us (2%)
  local copies, waits for them, and re-layouts  32.8 us (1%)
    ppermute x83, waiting for transfers between devices, hop(): lax.ppermute(value, 'data', [(i, i ^ mask) for i in range(self.size)])  1110 us
    pallas_call x30, Pallas kernels, run(): pl.pallas_call(kernel, grid_spec=pltpu.PrefetchScalarGridSpec(num_scalar_...  923 us
    dot_general x6, matrix products, share(): lax.dot_general(lhs, rhs, ROW_CONTRACT, preferred_element_type=jnp.float32)  120 us
    ppermute x83, starting transfers between devices, hop(): lax.ppermute(value, 'data', [(i, i ^ mask) for i in range(self.size)])  98.1 us
  transfers between devices with their start and end apart: 83, of which 30 were waited for; matrix products, arithmetic and copies ran while one was open for 8% of the time, Pallas kernels for 38%

profile of v2, /device:TPU:1, one launch (start us, length us, event | category | flops | bytes accessed | tf_op | source)
XLA Modules:
  0.0 2331.0 jit_solution(15779016519661303023)
XLA Ops:
  52.7 37.5 %shard_map.163 = (f32[512,8192]{1,0:T(8,128)}, bf16[512,2048]{1,0:T(8,128)(2,1)}, bf16[512,2048]{1,0:T(8,128)(2,1)}, bf16[512,2048]{1,0:T(8,128)(2,1)}, bf16[512,2048]{1,0:T(8,128)(2,1)}) custom-call(s32[8]{0:T(128)} %stack.137.table_ref, bf16[512,2048]{1,0:T(8,128)(2,1)} %get-tuple-element.107.p_ref, f32[2,2048,8192]{2,1,0:T(8,128)} %refs_2_.35), custom_call_target="tpu_custom_call" | custom-call | flops 17179869184 | bytes 92274688 | tf_op jit(solution)/shard_map/pallas_call | solution.py:75
  90.2 33.6 %shard_map.164 = (f32[512,2048]{1,0:T(8,128)}, bf16[512,2048]{1,0:T(8,128)(2,1)}) custom-call(s32[8]{0:T(128)} %stack.137.table_ref, f32[512,2048]{1,0:T(8,128)} %get-tuple-element.106.base_ref, f32[2,8192,2048]{2,1,0:T(8,128)} %refs_2_.39, bf16[512,2048]{1,0:T(8,128)(2,1)} %get-tuple-element.108.refs_0_, bf16[512,2048]{1,0:T(8,128)(2,1)} %get-tuple-element.109.refs_1_, ...), custom_call_target="tpu_custom_call" | custom-call | flops 17179869184 | bytes 75497472 | tf_op jit(solution)/shard_map/pallas_call | solution.py:75
  123.8 37.5 %shard_map.165 = (f32[512,8192]{1,0:T(8,128)}, bf16[512,2048]{1,0:T(8,128)(2,1)}, bf16[512,2048]{1,0:T(8,128)(2,1)}, bf16[512,2048]{1,0:T(8,128)(2,1)}, bf16[512,2048]{1,0:T(8,128)(2,1)}) custom-call(s32[8]{0:T(128)} %stack.128.table_ref, bf16[512,2048]{1,0:T(8,128)(2,1)} %get-tuple-element.113.p_ref, f32[2,2048,8192]{2,1,0:T(8,128)} %refs_2_.35), custom_call_target="tpu_custom_call" | custom-call | flops 17179869184 | bytes 92274688 | tf_op jit(solution)/shard_map/pallas_call | solution.py:75
  161.3 34.2 %shard_map.166 = (f32[512,2048]{1,0:T(8,128)}, bf16[512,2048]{1,0:T(8,128)(2,1)}) custom-call(s32[8]{0:T(128)} %stack.128.table_ref, f32[512,2048]{1,0:T(8,128)} %get-tuple-element.112.base_ref, f32[2,8192,2048]{2,1,0:T(8,128)} %refs_2_.39, bf16[512,2048]{1,0:T(8,128)(2,1)} %get-tuple-element.114.refs_0_, bf16[512,2048]{1,0:T(8,128)(2,1)} %get-tuple-element.115.refs_1_, ...), custom_call_target="tpu_custom_call" | custom-call | flops 17179869184 | bytes 75497472 | tf_op jit(solution)/shard_map/pallas_call | solution.py:75
  201.6 38.0 %shard_map.167 = (bf16[512,2048]{1,0:T(8,128)(2,1)}, bf16[512,2048]{1,0:T(8,128)(2,1)}, bf16[512,2048]{1,0:T(8,128)(2,1)}, bf16[512,2048]{1,0:T(8,128)(2,1)}) custom-call(s32[8]{0:T(128)} %stack.137.table_ref, bf16[512,2048]{1,0:T(8,128)(2,1)} %get-tuple-element.196.c_ref, f32[2,8192,2048]{2,1,0:T(8,128)} %refs_2_.39, f32[512,8192]{1,0:T(8,128)} %get-tuple-element.119.u_ref), custom_call_target="tpu_custom_call" | custom-call | flops 17179869184 | bytes 92274688 | tf_op jit(solution)/shard_map/pallas_call | solution.py:75
  239.6 33.9 %shard_map.168 = (f32[512,2048]{1,0:T(8,128)}, bf16[512,2048]{1,0:T(8,128)(2,1)}) custom-call(s32[8]{0:T(128)} %stack.137.table_ref, f32[512,2048]{1,0:T(8,128)} %get-tuple-element.197.base_ref, f32[2,2048,8192]{2,1,0:T(8,128)} %refs_2_.35, bf16[512,2048]{1,0:T(8,128)(2,1)} %get-tuple-element.120.refs_0_, bf16[512,2048]{1,0:T(8,128)(2,1)} %get-tuple-element.121.refs_1_, ...), custom_call_target="tpu_custom_call" | custom-call | flops 17179869184 | bytes 75497472 | tf_op jit(solution)/shard_map/pallas_call | solution.py:75
  273.5 38.3 %shard_map.169 = (bf16[512,2048]{1,0:T(8,128)(2,1)}, bf16[512,2048]{1,0:T(8,128)(2,1)}, bf16[512,2048]{1,0:T(8,128)(2,1)}, bf16[512,2048]{1,0:T(8,128)(2,1)}) custom-call(s32[8]{0:T(128)} %stack.128.table_ref, bf16[512,2048]{1,0:T(8,128)(2,1)} %get-tuple-element.125.c_ref, f32[2,8192,2048]{2,1,0:T(8,128)} %refs_2_.39, f32[512,8192]{1,0:T(8,128)} %get-tuple-element.126.u_ref), custom_call_target="tpu_custom_call" | custom-call | flops 17179869184 | bytes 92274688 | tf_op jit(solution)/shard_map/pallas_call | solution.py:75
  311.8 34.2 %shard_map.170 = (f32[512,2048]{1,0:T(8,128)}, bf16[512,2048]{1,0:T(8,128)(2,1)}) custom-call(s32[8]{0:T(128)} %stack.128.table_ref, f32[512,2048]{1,0:T(8,128)} %get-tuple-element.124.base_ref, f32[2,2048,8192]{2,1,0:T(8,128)} %refs_2_.35, bf16[512,2048]{1,0:T(8,128)(2,1)} %get-tuple-element.127.refs_0_, bf16[512,2048]{1,0:T(8,128)(2,1)} %get-tuple-element.128.refs_1_, ...), custom_call_target="tpu_custom_call" | custom-call | flops 17179869184 | bytes 75497472 | tf_op jit(solution)/shard_map/pallas_call | solution.py:75
  354.0 38.9 %collective-permute-done.4 = bf16[512,2048]{1,0:T(8,128)(2,1)} collective-permute-done((bf16[512,2048]{1,0:T(8,128)(2,1)}, bf16[512,2048]{1,0:T(8,128)(2,1)}, u32[]{:S(2)}, u32[]{:S(2)}) %collective-permute-start.4) | collective-permute-done | bytes 2097184 | tf_op jit(solution)/shard_map/ppermute | solution.py:43
  397.1 42.8 %collective-permute-done.32 = bf16[512,2048]{1,0:T(8,128)(2,1)} collective-permute-done((bf16[512,2048]{1,0:T(8,128)(2,1)}, bf16[512,2048]{1,0:T(8,128)(2,1)}, u32[]{:S(2)}, u32[]{:S(2)}) %collective-permute-start.32) | collective-permute-done | bytes 2097184 | tf_op jit(solution)/shard_map/ppermute | solution.py:43
  439.9 42.9 %collective-permute-done.31 = bf16[512,2048]{1,0:T(8,128)(2,1)} collective-permute-done((bf16[512,2048]{1,0:T(8,128)(2,1)}, bf16[512,2048]{1,0:T(8,128)(2,1)}, u32[]{:S(2)}, u32[]{:S(2)}) %collective-permute-start.31) | collective-permute-done | bytes 2097184 | tf_op jit(solution)/shard_map/ppermute | solution.py:43
  486.9 40.7 %collective-permute-done.28 = bf16[512,2048]{1,0:T(8,128)(2,1)} collective-permute-done((bf16[512,2048]{1,0:T(8,128)(2,1)S(1)}, bf16[512,2048]{1,0:T(8,128)(2,1)}, u32[]{:S(2)}, u32[]{:S(2)}) %collective-permute-start.28) | collective-permute-done | bytes 2097184 | tf_op jit(solution)/shard_map/ppermute | solution.py:43
  577.5 44.2 %collective-permute-done.42 = bf16[512,2048]{1,0:T(8,128)(2,1)} collective-permute-done((bf16[512,2048]{1,0:T(8,128)(2,1)}, bf16[512,2048]{1,0:T(8,128)(2,1)}, u32[]{:S(2)}, u32[]{:S(2)}) %collective-permute-start.42) | collective-permute-done | bytes 2097184 | tf_op jit(solution)/shard_map/ppermute | solution.py:43
  667.0 89.5 %collective-permute-done.56 = bf16[512,2048]{1,0:T(8,128)(2,1)} collective-permute-done((bf16[512,2048]{1,0:T(8,128)(2,1)S(1)}, bf16[512,2048]{1,0:T(8,128)(2,1)}, u32[]{:S(2)}, u32[]{:S(2)}) %collective-permute-start.56) | collective-permute-done | bytes 2097184 | tf_op jit(solution)/shard_map/ppermute | solution.py:43
  852.1 44.2 %collective-permute-done.71 = bf16[512,2048]{1,0:T(8,128)(2,1)} collective-permute-done((bf16[512,2048]{1,0:T(8,128)(2,1)}, bf16[512,2048]{1,0:T(8,128)(2,1)}, u32[]{:S(2)}, u32[]{:S(2)}) %collective-permute-start.71) | collective-permute-done | bytes 2097184 | tf_op jit(solution)/shard_map/ppermute | solution.py:43
  897.0 42.3 %collective-permute-done.70 = bf16[512,2048]{1,0:T(8,128)(2,1)} collective-permute-done((bf16[512,2048]{1,0:T(8,128)(2,1)}, bf16[512,2048]{1,0:T(8,128)(2,1)}, u32[]{:S(2)}, u32[]{:S(2)}) %collective-permute-start.70) | collective-permute-done | bytes 2097184 | tf_op jit(solution)/shard_map/ppermute | solution.py:43
  971.6 58.4 %collective-permute-done.16.refs_6_ = bf16[512,2048]{1,0:T(8,128)(2,1)} collective-permute-done((bf16[512,2048]{1,0:T(8,128)(2,1)}, bf16[512,2048]{1,0:T(8,128)(2,1)}, u32[]{:S(2)}, u32[]{:S(2)}) %collective-permute-start.16) | collective-permute-done | bytes 2097184 | tf_op jit(solution)/shard_map/ppermute | solution.py:43
  1063.9 40.1 %collective-permute-done.23.refs_7_ = bf16[512,2048]{1,0:T(8,128)(2,1)} collective-permute-done((bf16[512,2048]{1,0:T(8,128)(2,1)}, bf16[512,2048]{1,0:T(8,128)(2,1)}, u32[]{:S(2)}, u32[]{:S(2)}) %collective-permute-start.23) | collective-permute-done | bytes 2097184 | tf_op jit(solution)/shard_map/ppermute | solution.py:43
  1124.3 85.5 %collective-permute-done.61 = bf16[2048,1024]{1,0:T(8,128)(2,1)} collective-permute-done((bf16[2048,1024]{1,0:T(8,128)(2,1)}, bf16[2048,1024]{1,0:T(8,128)(2,1)}, u32[]{:S(2)}, u32[]{:S(2)}) %collective-permute-start.61) | collective-permute-done | bytes 4194336 | tf_op jit(solution)/shard_map/ppermute | solution.py:43
  1288.6 61.2 %collective-permute-done.34.refs_4_ = bf16[2048,1024]{1,0:T(8,128)(2,1)} collective-permute-done((bf16[2048,1024]{1,0:T(8,128)(2,1)S(1)}, bf16[2048,1024]{1,0:T(8,128)(2,1)}, u32[]{:S(2)}, u32[]{:S(2)}) %collective-permute-start.34) | collective-permute-done | bytes 4194336 | tf_op jit(solution)/shard_map/ppermute | solution.py:43
  1360.0 88.5 %collective-permute-done.48.refs_4_ = bf16[1024,2048]{1,0:T(8,128)(2,1)} collective-permute-done((bf16[1024,2048]{1,0:T(8,128)(2,1)S(1)}, bf16[1024,2048]{1,0:T(8,128)(2,1)}, u32[]{:S(2)}, u32[]{:S(2)}) %collective-permute-start.48) | collective-permute-done | bytes 4194336 | tf_op jit(solution)/shard_map/ppermute | solution.py:43
  1454.3 84.1 %collective-permute-done.62.refs_4_ = bf16[2048,1024]{1,0:T(8,128)(2,1)} collective-permute-done((bf16[2048,1024]{1,0:T(8,128)(2,1)S(1)}, bf16[2048,1024]{1,0:T(8,128)(2,1)}, u32[]{:S(2)}, u32[]{:S(2)}) %collective-permute-start.62) | collective-permute-done | bytes 4194336 | tf_op jit(solution)/shard_map/ppermute | solution.py:43
  1544.0 84.6 %collective-permute-done.76.refs_4_ = bf16[1024,2048]{1,0:T(8,128)(2,1)} collective-permute-done((bf16[1024,2048]{1,0:T(8,128)(2,1)S(1)}, bf16[1024,2048]{1,0:T(8,128)(2,1)}, u32[]{:S(2)}, u32[]{:S(2)}) %collective-permute-start.76) | collective-permute-done | bytes 4194336 | tf_op jit(solution)/shard_map/ppermute | solution.py:43
  1652.1 74.8 %collective-permute-done.35.refs_4_ = bf16[2048,1024]{1,0:T(8,128)(2,1)} collective-permute-done((bf16[2048,1024]{1,0:T(8,128)(2,1)}, bf16[2048,1024]{1,0:T(8,128)(2,1)}, u32[]{:S(2)}, u32[]{:S(2)}) %collective-permute-start.35) | collective-permute-done | bytes 4194336 | tf_op jit(solution)/shard_map/ppermute | solution.py:43
  (264 shorter events, 1079.7 us)
Async XLA Ops:
  15.6 330.5 %collective-permute-start.2 = (bf16[512,1024]{1,0:T(8,128)(2,1)}, bf16[512,1024]{1,0:T(8,128)(2,1)}, u32[]{:S(2)}, u32[]{:S(2)}) collective-permute-start(bf16[512,1024]{1,0:T(8,128)(2,1)} %get-tuple-element.105), channel_id=1, source_target_pairs={{0,3},{1,2},{2,1},{3,0},{4,7},{5,6},{6,5},{7,4}} | collective-permute-start | bytes 3145736 | tf_op jit(solution)/shard_map/ppermute | solution.py:43
  18.2 329.3 %collective-permute-start.1 = (bf16[512,1024]{1,0:T(8,128)(2,1)}, bf16[512,1024]{1,0:T(8,128)(2,1)}, u32[]{:S(2)}, u32[]{:S(2)}) collective-permute-start(bf16[512,1024]{1,0:T(8,128)(2,1)} %get-tuple-element.104), channel_id=1, source_target_pairs={{0,2},{1,3},{2,0},{3,1},{4,6},{5,7},{6,4},{7,5}} | collective-permute-start | bytes 3145736 | tf_op jit(solution)/shard_map/ppermute | solution.py:43
  18.2 330.0 %collective-permute-start = (bf16[512,1024]{1,0:T(8,128)(2,1)}, bf16[512,1024]{1,0:T(8,128)(2,1)}, u32[]{:S(2)}, u32[]{:S(2)}) collective-permute-start(bf16[512,1024]{1,0:T(8,128)(2,1)} %get-tuple-element.103), channel_id=1, source_target_pairs={{0,1},{1,0},{2,3},{3,2},{4,5},{5,4},{6,7},{7,6}} | collective-permute-start | bytes 3145736 | tf_op jit(solution)/shard_map/ppermute | solution.py:43
  18.6 330.8 %collective-permute-start.12 = (bf16[512,1024]{1,0:T(8,128)(2,1)}, bf16[512,1024]{1,0:T(8,128)(2,1)}, u32[]{:S(2)}, u32[]{:S(2)}) collective-permute-start(bf16[512,1024]{1,0:T(8,128)(2,1)} %get-tuple-element.135), channel_id=1, source_target_pairs={{0,5},{1,4},{2,7},{3,6},{4,1},{5,0},{6,3},{7,2}} | collective-permute-start | bytes 3145736 | tf_op jit(solution)/shard_map/ppermute | solution.py:43
  20.1 329.9 %collective-permute-start.11 = (bf16[512,1024]{1,0:T(8,128)(2,1)}, bf16[512,1024]{1,0:T(8,128)(2,1)}, u32[]{:S(2)}, u32[]{:S(2)}) collective-permute-start(bf16[512,1024]{1,0:T(8,128)(2,1)} %get-tuple-element.134), channel_id=1, source_target_pairs={{0,4},{1,5},{2,6},{3,7},{4,0},{5,1},{6,2},{7,3}} | collective-permute-start | bytes 3145736 | tf_op jit(solution)/shard_map/ppermute | solution.py:43
  577.1 180.1 %collective-permute-start.59 = (bf16[512,2048]{1,0:T(8,128)(2,1)}, bf16[512,2048]{1,0:T(8,128)(2,1)}, u32[]{:S(2)}, u32[]{:S(2)}) collective-permute-start(bf16[512,2048]{1,0:T(8,128)(2,1)} %get-tuple-element.120.refs_0_), channel_id=1, source_target_pairs={{0,4},{1,5},{2,6},{3,7},{4,0},{5,1},{6,2},{7,3}} | collective-permute-start | bytes 6291464 | tf_op jit(solution)/shard_map/ppermute | solution.py:43
  971.6 238.2 %collective-permute-start.61 = (bf16[2048,1024]{1,0:T(8,128)(2,1)}, bf16[2048,1024]{1,0:T(8,128)(2,1)}, u32[]{:S(2)}, u32[]{:S(2)}) collective-permute-start(bf16[2048,1024]{1,0:T(8,128)(2,1)} %constant_dynamic-slice_fusion.1), channel_id=1, source_target_pairs={{0,2},{1,3},{2,0},{3,1},{4,6},{5,7},{6,4},{7,5}} | collective-permute-start | bytes 12582920 | tf_op jit(solution)/shard_map/ppermute | solution.py:43
  1269.8 178.7 %collective-permute-start.48 = (bf16[1024,2048]{1,0:T(8,128)(2,1)S(1)}, bf16[1024,2048]{1,0:T(8,128)(2,1)}, u32[]{:S(2)}, u32[]{:S(2)}) collective-permute-start(bf16[1024,2048]{1,0:T(8,128)(2,1)S(1)} %add_convert_fusion.2.refs_4_), channel_id=1, source_target_pairs={{0,2},{1,3},{2,0},{3,1},{4,6},{5,7},{6,4},{7,5}} | collective-permute-start | bytes 12582920 | tf_op jit(solution)/shard_map/ppermute | solution.py:43
  1273.1 176.9 %collective-permute-start.52 = (bf16[1024,2048]{1,0:T(8,128)(2,1)S(1)}, bf16[1024,2048]{1,0:T(8,128)(2,1)}, u32[]{:S(2)}, u32[]{:S(2)}) collective-permute-start(bf16[1024,2048]{1,0:T(8,128)(2,1)S(1)} %add_convert_fusion.2.refs_4_), channel_id=1, source_target_pairs={{0,4},{1,5},{2,6},{3,7},{4,0},{5,1},{6,2},{7,3}} | collective-permute-start | bytes 12582920 | tf_op jit(solution)/shard_map/ppermute | solution.py:43
  1282.2 167.8 %collective-permute-start.68 = (bf16[2048,1024]{1,0:T(8,128)(2,1)S(1)}, bf16[2048,1024]{1,0:T(8,128)(2,1)S(1)}, u32[]{:S(2)}, u32[]{:S(2)}) collective-permute-start(bf16[2048,1024]{1,0:T(8,128)(2,1)S(1)} %add_convert_fusion.1.refs_4_), channel_id=1, source_target_pairs={{0,1},{1,0},{2,3},{3,2},{4,5},{5,4},{6,7},{7,6}} | collective-permute-start | bytes 12582920 | tf_op jit(solution)/shard_map/ppermute | solution.py:43
  1358.7 179.8 %collective-permute-start.62 = (bf16[2048,1024]{1,0:T(8,128)(2,1)S(1)}, bf16[2048,1024]{1,0:T(8,128)(2,1)}, u32[]{:S(2)}, u32[]{:S(2)}) collective-permute-start(bf16[2048,1024]{1,0:T(8,128)(2,1)S(1)} %add_convert_fusion.1.refs_4_), channel_id=1, source_target_pairs={{0,2},{1,3},{2,0},{3,1},{4,6},{5,7},{6,4},{7,5}} | collective-permute-start | bytes 12582920 | tf_op jit(solution)/shard_map/ppermute | solution.py:43
  1450.0 178.6 %collective-permute-start.76 = (bf16[1024,2048]{1,0:T(8,128)(2,1)S(1)}, bf16[1024,2048]{1,0:T(8,128)(2,1)}, u32[]{:S(2)}, u32[]{:S(2)}) collective-permute-start(bf16[1024,2048]{1,0:T(8,128)(2,1)S(1)} %add_convert_fusion.refs_4_), channel_id=1, source_target_pairs={{0,4},{1,5},{2,6},{3,7},{4,0},{5,1},{6,2},{7,3}} | collective-permute-start | bytes 12582920 | tf_op jit(solution)/shard_map/ppermute | solution.py:43
  1450.0 181.5 %collective-permute-start.80 = (bf16[1024,2048]{1,0:T(8,128)(2,1)S(1)}, bf16[1024,2048]{1,0:T(8,128)(2,1)S(1)}, u32[]{:S(2)}, u32[]{:S(2)}) collective-permute-start(bf16[1024,2048]{1,0:T(8,128)(2,1)S(1)} %add_convert_fusion.refs_4_), channel_id=1, source_target_pairs={{0,2},{1,3},{2,0},{3,1},{4,6},{5,7},{6,4},{7,5}} | collective-permute-start | bytes 12582920 | tf_op jit(solution)/shard_map/ppermute | solution.py:43
  1451.5 184.8 %collective-permute-start.37 = (bf16[2048,1024]{1,0:T(8,128)(2,1)}, bf16[2048,1024]{1,0:T(8,128)(2,1)}, u32[]{:S(2)}, u32[]{:S(2)}) collective-permute-start(bf16[2048,1024]{1,0:T(8,128)(2,1)} %collective-permute-done.34.refs_4_), channel_id=1, source_target_pairs={{0,1},{1,0},{2,3},{3,2},{4,5},{5,4},{6,7},{7,6}} | collective-permute-start | bytes 12582920 | tf_op jit(solution)/shard_map/ppermute | solution.py:43
  1638.6 247.7 %collective-permute-start.65 = (bf16[2048,1024]{1,0:T(8,128)(2,1)}, bf16[2048,1024]{1,0:T(8,128)(2,1)}, u32[]{:S(2)}, u32[]{:S(2)}) collective-permute-start(bf16[2048,1024]{1,0:T(8,128)(2,1)} %collective-permute-done.62.refs_4_), channel_id=1, source_target_pairs={{0,1},{1,0},{2,3},{3,2},{4,5},{5,4},{6,7},{7,6}} | collective-permute-start | bytes 12582920 | tf_op jit(solution)/shard_map/ppermute | solution.py:43
  1644.6 272.1 %collective-permute-start.63 = (bf16[2048,1024]{1,0:T(8,128)(2,1)}, bf16[2048,1024]{1,0:T(8,128)(2,1)}, u32[]{:S(2)}, u32[]{:S(2)}) collective-permute-start(bf16[2048,1024]{1,0:T(8,128)(2,1)} %collective-permute-done.62.refs_4_), channel_id=1, source_target_pairs={{0,4},{1,5},{2,6},{3,7},{4,0},{5,1},{6,2},{7,3}} | collective-permute-start | bytes 12582920 | tf_op jit(solution)/shard_map/ppermute | solution.py:43
  1650.6 266.7 %collective-permute-start.77 = (bf16[1024,2048]{1,0:T(8,128)(2,1)}, bf16[1024,2048]{1,0:T(8,128)(2,1)}, u32[]{:S(2)}, u32[]{:S(2)}) collective-permute-start(bf16[1024,2048]{1,0:T(8,128)(2,1)} %collective-permute-done.76.refs_4_), channel_id=1, source_target_pairs={{0,2},{1,3},{2,0},{3,1},{4,6},{5,7},{6,4},{7,5}} | collective-permute-start | bytes 12582920 | tf_op jit(solution)/shard_map/ppermute | solution.py:43
  1726.8 218.5 %collective-permute-start.36 = (bf16[2048,1024]{1,0:T(8,128)(2,1)}, bf16[2048,1024]{1,0:T(8,128)(2,1)}, u32[]{:S(2)}, u32[]{:S(2)}) collective-permute-start(bf16[2048,1024]{1,0:T(8,128)(2,1)} %collective-permute-done.35.refs_4_), channel_id=1, source_target_pairs={{0,1},{1,0},{2,3},{3,2},{4,5},{5,4},{6,7},{7,6}} | collective-permute-start | bytes 12582920 | tf_op jit(solution)/shard_map/ppermute | solution.py:43
  1729.8 246.5 %collective-permute-start.50 = (bf16[1024,2048]{1,0:T(8,128)(2,1)}, bf16[1024,2048]{1,0:T(8,128)(2,1)}, u32[]{:S(2)}, u32[]{:S(2)}) collective-permute-start(bf16[1024,2048]{1,0:T(8,128)(2,1)} %collective-permute-done.49.refs_4_), channel_id=1, source_target_pairs={{0,1},{1,0},{2,3},{3,2},{4,5},{5,4},{6,7},{7,6}} | collective-permute-start | bytes 12582920 | tf_op jit(solution)/shard_map/ppermute | solution.py:43
  1886.4 323.9 %collective-permute-start.67 = (bf16[2048,1024]{1,0:T(8,128)(2,1)}, bf16[2048,1024]{1,0:T(8,128)(2,1)}, u32[]{:S(2)}, u32[]{:S(2)}) collective-permute-start(bf16[2048,1024]{1,0:T(8,128)(2,1)} %copy-done.7), channel_id=1, source_target_pairs={{0,1},{1,0},{2,3},{3,2},{4,5},{5,4},{6,7},{7,6}} | collective-permute-start | bytes 12582920 | tf_op jit(solution)/shard_map/ppermute | solution.py:43
  1916.8 321.5 %collective-permute-start.79 = (bf16[1024,2048]{1,0:T(8,128)(2,1)}, bf16[1024,2048]{1,0:T(8,128)(2,1)}, u32[]{:S(2)}, u32[]{:S(2)}) collective-permute-start(bf16[1024,2048]{1,0:T(8,128)(2,1)} %collective-permute-done.76.refs_4_), channel_id=1, source_target_pairs={{0,1},{1,0},{2,3},{3,2},{4,5},{5,4},{6,7},{7,6}} | collective-permute-start | bytes 12582920 | tf_op jit(solution)/shard_map/ppermute | solution.py:43
  1917.3 321.0 %collective-permute-start.81 = (bf16[1024,2048]{1,0:T(8,128)(2,1)}, bf16[1024,2048]{1,0:T(8,128)(2,1)}, u32[]{:S(2)}, u32[]{:S(2)}) collective-permute-start(bf16[1024,2048]{1,0:T(8,128)(2,1)} %copy-done.6), channel_id=1, source_target_pairs={{0,1},{1,0},{2,3},{3,2},{4,5},{5,4},{6,7},{7,6}} | collective-permute-start | bytes 12582920 | tf_op jit(solution)/shard_map/ppermute | solution.py:43
  1945.4 323.4 %collective-permute-start.64 = (bf16[2048,1024]{1,0:T(8,128)(2,1)}, bf16[2048,1024]{1,0:T(8,128)(2,1)}, u32[]{:S(2)}, u32[]{:S(2)}) collective-permute-start(bf16[2048,1024]{1,0:T(8,128)(2,1)} %collective-permute-done.63.refs_4_), channel_id=1, source_target_pairs={{0,1},{1,0},{2,3},{3,2},{4,5},{5,4},{6,7},{7,6}} | collective-permute-start | bytes 12582920 | tf_op jit(solution)/shard_map/ppermute | solution.py:43
  1976.3 320.6 %collective-permute-start.78 = (bf16[1024,2048]{1,0:T(8,128)(2,1)}, bf16[1024,2048]{1,0:T(8,128)(2,1)}, u32[]{:S(2)}, u32[]{:S(2)}) collective-permute-start(bf16[1024,2048]{1,0:T(8,128)(2,1)} %collective-permute-done.77.refs_4_), channel_id=1, source_target_pairs={{0,1},{1,0},{2,3},{3,2},{4,5},{5,4},{6,7},{7,6}} | collective-permute-start | bytes 12582920 | tf_op jit(solution)/shard_map/ppermute | solution.py:43
  (88 other events, 6956.7 us)
